TPU v7x, 256 devices: a whole 4x4x8 slice. The times are simulated.
256 devices in a mesh: seq: 64 (over z, x_hi, y), head: 4 (over x_lo, core).
Axes of the slice: x: 4 (x_hi: 2, x_lo: 2; x = x_hi * 2 + x_lo), y: 4, z: 8, core: 2. Of those that a mesh axis runs over, the one named last changes fastest.
Arguments:
- queries: bfloat16 [16384, 32, 128], P('seq', 'head'), may hold values from -160 to 160
- keys: bfloat16 [16384, 8, 128], P('seq', 'head'), may hold values from -7 to 7
- values: bfloat16 [16384, 8, 128], P('seq', 'head'), may hold values from -6 to 6
- out_weight: bfloat16 [4096, 4096], P('head', 'seq'), may hold values from -0.75 to 0.75
Outputs:
- mixed: bfloat16 [16384, 4096], P('seq', 'head')
All inputs are finite; a program needn't handle non-finite values.
Results may differ from a plain program's by a relative error of at most 0.013.
Values may be sent and summed in bfloat16 or wider, within the bound.
A program may use at most 64 MiB of HBM per device.

v0:
```python
import jax
import jax.numpy as jnp
from jax import lax
from jax.sharding import PartitionSpec as P

ATTENTION_SPAN = 4096


def from_behind(shard, axis, by):
    devices = lax.axis_size(axis)
    pairs = [(i, i + by) for i in range(devices) if 0 <= i + by < devices]
    return lax.ppermute(shard, axis, pairs)


def in_blocks(shard, dim, devices):
    before, after = (shard.shape[:dim], shard.shape[dim + 1 :])
    return jnp.moveaxis(shard.reshape(*before, devices, -1, *after), dim, 0)


def sent_and_summed(shard, axis, dim):
    devices = lax.axis_size(axis)
    tiles = lax.all_to_all(in_blocks(shard, dim, devices), axis, 0, 0, tiled=True)
    return jnp.sum(tiles.astype(jnp.float32), axis=0)


def body(queries, keys, values, out_weight):
    shard_rows = queries.shape[0]
    query_heads = queries.shape[1]
    head_dim = queries.shape[2]
    kv_heads = keys.shape[1]
    query_group_width = query_heads // kv_heads
    score_scale = head_dim ** (-0.5)
    hop_count = min(ATTENTION_SPAN // shard_rows, lax.axis_size("seq") - 1)
    seq_index = lax.axis_index("seq")
    grouped = queries.reshape(shard_rows, kv_heads, query_group_width, head_dim)
    query_pos = seq_index * shard_rows + jnp.arange(shard_rows, dtype=jnp.int32)

    def absorb(carried, block_keys, block_values, key_start):
        running_max, running_sum, numerator = carried
        key_pos = key_start + jnp.arange(shard_rows, dtype=jnp.int32)
        distance = query_pos[:, None] - key_pos[None, :]
        inside = (distance >= 0) & (distance < ATTENTION_SPAN) & (key_pos >= 0)[None, :]
        scores = (
            jnp.einsum("tkgd,skd->kgts", grouped, block_keys, preferred_element_type=jnp.float32)
            * score_scale
        )
        scores = jnp.where(inside, scores, -1e30)
        new_max = jnp.maximum(running_max, jnp.max(scores, axis=-1))
        weights = jnp.where(inside, jnp.exp(scores - new_max[..., None]), 0.0)
        rescale = jnp.exp(running_max - new_max)
        running_sum = running_sum * rescale + jnp.sum(weights, axis=-1)
        update = jnp.einsum(
            "kgts,skd->kgtd",
            weights.astype(jnp.bfloat16),
            block_values,
            preferred_element_type=jnp.float32,
        )
        numerator = numerator * rescale[..., None] + update
        return (new_max, running_sum, numerator)

    blank = (
        jnp.full((kv_heads, query_group_width, shard_rows), -1e30, jnp.float32),
        jnp.zeros((kv_heads, query_group_width, shard_rows), jnp.float32),
        jnp.zeros((kv_heads, query_group_width, shard_rows, head_dim), jnp.float32),
    )
    carried = absorb(blank, keys, values, seq_index * shard_rows)
    for hop_index in range(1, hop_count + 1):
        fetched = from_behind((keys, values), "seq", hop_index)
        carried = absorb(carried, fetched[0], fetched[1], (seq_index - hop_index) * shard_rows)
    running_max, running_sum, numerator = carried
    result = numerator / running_sum[..., None]
    attended = (
        jnp.transpose(result, (2, 0, 1, 3))
        .reshape(shard_rows, query_heads * head_dim)
        .astype(jnp.bfloat16)
    )
    partials = jnp.dot(
        attended,
        lax.all_gather(out_weight, "seq", axis=1, tiled=True),
        preferred_element_type=jnp.float32,
    )
    own_columns = sent_and_summed(partials.astype(jnp.bfloat16), "head", 1)
    return own_columns.astype(jnp.bfloat16)


def solution(mesh):
    return jax.shard_map(
        body,
        mesh=mesh,
        in_specs=(
            P("seq", "head", None),
            P("seq", "head", None),
            P("seq", "head", None),
            P("head", "seq"),
        ),
        out_specs=P("seq", "head"),
        check_vma=False,
    )
```

profile of v0, /device:TPU:1, one launch (start us, length us, event | category | flops | bytes accessed | tf_op | source)
XLA Modules:
  0.0 269.2 jit_solution(14719325698131183841)
XLA Ops:
  7.5 7.0 %collective-permute-start.18 = (bf16[256,2,128]{2,0,1:T(8,128)(2,1)S(1)}, bf16[256,2,128]{2,0,1:T(8,128)(2,1)S(1)}, u32[]{:S(2)}, u32[]{:S(2)}) collective-permute-start(bf16[256,2,128]{2,0,1:T(8,128)(2,1)S(1)} %copy.77), channel_id=1, source_target_pairs={{0,40},{4,44},{8,48},{12,52},{16,56},{20,60},{24,64},{28,68},{32,7... | collective-permute-start | bytes 393224 | tf_op jit(solution)/shard_map/ppermute | solution.py:12
  14.5 3.7 %collective-permute-start.16 = (bf16[256,2,128]{2,0,1:T(8,128)(2,1)S(1)}, bf16[256,2,128]{2,0,1:T(8,128)(2,1)S(1)}, u32[]{:S(2)}, u32[]{:S(2)}) collective-permute-start(bf16[256,2,128]{2,0,1:T(8,128)(2,1)S(1)} %copy.77), channel_id=1, source_target_pairs={{0,36},{4,40},{8,44},{12,48},{16,52},{20,56},{24,60},{28,64},{32,6... | collective-permute-start | bytes 393224 | tf_op jit(solution)/shard_map/ppermute | solution.py:12
  18.2 3.5 %collective-permute-start.14 = (bf16[256,2,128]{2,0,1:T(8,128)(2,1)S(1)}, bf16[256,2,128]{2,0,1:T(8,128)(2,1)S(1)}, u32[]{:S(2)}, u32[]{:S(2)}) collective-permute-start(bf16[256,2,128]{2,0,1:T(8,128)(2,1)S(1)} %copy.77), channel_id=1, source_target_pairs={{0,32},{4,36},{8,40},{12,44},{16,48},{20,52},{24,56},{28,60},{32,6... | collective-permute-start | bytes 393224 | tf_op jit(solution)/shard_map/ppermute | solution.py:12
  21.8 9.2 %collective-permute-start.12 = (bf16[256,2,128]{2,0,1:T(8,128)(2,1)S(1)}, bf16[256,2,128]{2,0,1:T(8,128)(2,1)S(1)}, u32[]{:S(2)}, u32[]{:S(2)}) collective-permute-start(bf16[256,2,128]{2,0,1:T(8,128)(2,1)S(1)} %copy.77), channel_id=1, source_target_pairs={{0,28},{4,32},{8,36},{12,40},{16,44},{20,48},{24,52},{28,56},{32,6... | collective-permute-start | bytes 393224 | tf_op jit(solution)/shard_map/ppermute | solution.py:12
  37.8 5.6 %collective-permute-start.8 = (bf16[256,2,128]{2,0,1:T(8,128)(2,1)S(1)}, bf16[256,2,128]{2,0,1:T(8,128)(2,1)S(1)}, u32[]{:S(2)}, u32[]{:S(2)}) collective-permute-start(bf16[256,2,128]{2,0,1:T(8,128)(2,1)S(1)} %copy.77), channel_id=1, source_target_pairs={{0,20},{4,24},{8,28},{12,32},{16,36},{20,40},{24,44},{28,48},{32,5... | collective-permute-start | bytes 393224 | tf_op jit(solution)/shard_map/ppermute | solution.py:12
  46.9 4.1 %collective-permute-start.4 = (bf16[256,2,128]{2,0,1:T(8,128)(2,1)S(1)}, bf16[256,2,128]{2,0,1:T(8,128)(2,1)S(1)}, u32[]{:S(2)}, u32[]{:S(2)}) collective-permute-start(bf16[256,2,128]{2,0,1:T(8,128)(2,1)S(1)} %copy.77), channel_id=1, source_target_pairs={{0,12},{4,16},{8,20},{12,24},{16,28},{20,32},{24,36},{28,40},{32,4... | collective-permute-start | bytes 393224 | tf_op jit(solution)/shard_map/ppermute | solution.py:12
  51.5 3.1 %collective-permute-start.30 = (bf16[256,2,128]{2,0,1:T(8,128)(2,1)S(1)}, bf16[256,2,128]{2,0,1:T(8,128)(2,1)S(1)}, u32[]{:S(2)}, u32[]{:S(2)}) collective-permute-start(bf16[256,2,128]{2,0,1:T(8,128)(2,1)S(1)} %copy.77), channel_id=1, source_target_pairs={{0,64},{4,68},{8,72},{12,76},{16,80},{20,84},{24,88},{28,92},{32,9... | collective-permute-start | bytes 393224 | tf_op jit(solution)/shard_map/ppermute | solution.py:12
  55.1 4.0 %collective-permute-start.28 = (bf16[256,2,128]{2,0,1:T(8,128)(2,1)S(1)}, bf16[256,2,128]{2,0,1:T(8,128)(2,1)S(1)}, u32[]{:S(2)}, u32[]{:S(2)}) collective-permute-start(bf16[256,2,128]{2,0,1:T(8,128)(2,1)S(1)} %copy.77), channel_id=1, source_target_pairs={{0,60},{4,64},{8,68},{12,72},{16,76},{20,80},{24,84},{28,88},{32,9... | collective-permute-start | bytes 393224 | tf_op jit(solution)/shard_map/ppermute | solution.py:12
  65.1 3.1 %collective-permute-start.22 = (bf16[256,2,128]{2,0,1:T(8,128)(2,1)S(1)}, bf16[256,2,128]{2,0,1:T(8,128)(2,1)S(1)}, u32[]{:S(2)}, u32[]{:S(2)}) collective-permute-start(bf16[256,2,128]{2,0,1:T(8,128)(2,1)S(1)} %copy.77), channel_id=1, source_target_pairs={{0,48},{4,52},{8,56},{12,60},{16,64},{20,68},{24,72},{28,76},{32,8... | collective-permute-start | bytes 393224 | tf_op jit(solution)/shard_map/ppermute | solution.py:12
  70.6 4.3 %collective-permute-start.2 = (bf16[256,2,128]{2,0,1:T(8,128)(2,1)S(1)}, bf16[256,2,128]{2,0,1:T(8,128)(2,1)S(1)}, u32[]{:S(2)}, u32[]{:S(2)}) collective-permute-start(bf16[256,2,128]{2,0,1:T(8,128)(2,1)S(1)} %copy.77), channel_id=1, source_target_pairs={{0,8},{4,12},{8,16},{12,20},{16,24},{20,28},{24,32},{28,36},{32,40... | collective-permute-start | bytes 393224 | tf_op jit(solution)/shard_map/ppermute | solution.py:12
  77.4 5.8 %collective-permute-start.11 = (bf16[256,2,128]{0,2,1:T(8,128)(2,1)}, bf16[256,2,128]{0,2,1:T(8,128)(2,1)S(1)}, u32[]{:S(2)}, u32[]{:S(2)}) collective-permute-start(bf16[256,2,128]{0,2,1:T(8,128)(2,1)} %copy.79), channel_id=1, source_target_pairs={{0,24},{4,28},{8,32},{12,36},{16,40},{20,44},{24,48},{28,52},{32,5... | collective-permute-start | bytes 393224 | tf_op jit(solution)/shard_map/ppermute | solution.py:12
  83.7 10.3 %collective-permute-start.9 = (bf16[256,2,128]{0,2,1:T(8,128)(2,1)}, bf16[256,2,128]{0,2,1:T(8,128)(2,1)S(1)}, u32[]{:S(2)}, u32[]{:S(2)}) collective-permute-start(bf16[256,2,128]{0,2,1:T(8,128)(2,1)} %copy.79), channel_id=1, source_target_pairs={{0,20},{4,24},{8,28},{12,32},{16,36},{20,40},{24,44},{28,48},{32,5... | collective-permute-start | bytes 393224 | tf_op jit(solution)/shard_map/ppermute | solution.py:12
  99.0 8.5 %collective-permute-start.19 = (bf16[256,2,128]{0,2,1:T(8,128)(2,1)}, bf16[256,2,128]{0,2,1:T(8,128)(2,1)S(1)}, u32[]{:S(2)}, u32[]{:S(2)}) collective-permute-start(bf16[256,2,128]{0,2,1:T(8,128)(2,1)} %copy.79), channel_id=1, source_target_pairs={{0,40},{4,44},{8,48},{12,52},{16,56},{20,60},{24,64},{28,68},{32,7... | collective-permute-start | bytes 393224 | tf_op jit(solution)/shard_map/ppermute | solution.py:12
  108.8 3.0 %collective-permute-start.17 = (bf16[256,2,128]{0,2,1:T(8,128)(2,1)}, bf16[256,2,128]{0,2,1:T(8,128)(2,1)S(1)}, u32[]{:S(2)}, u32[]{:S(2)}) collective-permute-start(bf16[256,2,128]{0,2,1:T(8,128)(2,1)} %copy.79), channel_id=1, source_target_pairs={{0,36},{4,40},{8,44},{12,48},{16,52},{20,56},{24,60},{28,64},{32,6... | collective-permute-start | bytes 393224 | tf_op jit(solution)/shard_map/ppermute | solution.py:12
  112.6 3.5 %collective-permute-start.15 = (bf16[256,2,128]{0,2,1:T(8,128)(2,1)}, bf16[256,2,128]{0,2,1:T(8,128)(2,1)S(1)}, u32[]{:S(2)}, u32[]{:S(2)}) collective-permute-start(bf16[256,2,128]{0,2,1:T(8,128)(2,1)} %copy.79), channel_id=1, source_target_pairs={{0,32},{4,36},{8,40},{12,44},{16,48},{20,52},{24,56},{28,60},{32,6... | collective-permute-start | bytes 393224 | tf_op jit(solution)/shard_map/ppermute | solution.py:12
  116.8 7.3 %collective-permute-start.13 = (bf16[256,2,128]{0,2,1:T(8,128)(2,1)}, bf16[256,2,128]{0,2,1:T(8,128)(2,1)S(1)}, u32[]{:S(2)}, u32[]{:S(2)}) collective-permute-start(bf16[256,2,128]{0,2,1:T(8,128)(2,1)} %copy.79), channel_id=1, source_target_pairs={{0,28},{4,32},{8,36},{12,40},{16,44},{20,48},{24,52},{28,56},{32,6... | collective-permute-start | bytes 393224 | tf_op jit(solution)/shard_map/ppermute | solution.py:12
  126.9 2.8 %collective-permute-start.25 = (bf16[256,2,128]{0,2,1:T(8,128)(2,1)}, bf16[256,2,128]{0,2,1:T(8,128)(2,1)S(1)}, u32[]{:S(2)}, u32[]{:S(2)}) collective-permute-start(bf16[256,2,128]{0,2,1:T(8,128)(2,1)} %copy.79), channel_id=1, source_target_pairs={{0,52},{4,56},{8,60},{12,64},{16,68},{20,72},{24,76},{28,80},{32,8... | collective-permute-start | bytes 393224 | tf_op jit(solution)/shard_map/ppermute | solution.py:12
  135.5 4.3 %collective-permute-start.27 = (bf16[256,2,128]{0,2,1:T(8,128)(2,1)}, bf16[256,2,128]{0,2,1:T(8,128)(2,1)S(1)}, u32[]{:S(2)}, u32[]{:S(2)}) collective-permute-start(bf16[256,2,128]{0,2,1:T(8,128)(2,1)} %copy.79), channel_id=1, source_target_pairs={{0,56},{4,60},{8,64},{12,68},{16,72},{20,76},{24,80},{28,84},{32,8... | collective-permute-start | bytes 393224 | tf_op jit(solution)/shard_map/ppermute | solution.py:12
  140.5 17.8 %collective-permute-start.29 = (bf16[256,2,128]{0,2,1:T(8,128)(2,1)}, bf16[256,2,128]{0,2,1:T(8,128)(2,1)S(1)}, u32[]{:S(2)}, u32[]{:S(2)}) collective-permute-start(bf16[256,2,128]{0,2,1:T(8,128)(2,1)} %copy.79), channel_id=1, source_target_pairs={{0,60},{4,64},{8,68},{12,72},{16,76},{20,80},{24,84},{28,88},{32,9... | collective-permute-start | bytes 393224 | tf_op jit(solution)/shard_map/ppermute | solution.py:12
  161.1 5.7 %collective-permute-start.1 = (bf16[256,2,128]{0,2,1:T(8,128)(2,1)}, bf16[256,2,128]{0,2,1:T(8,128)(2,1)}, u32[]{:S(2)}, u32[]{:S(2)}) collective-permute-start(bf16[256,2,128]{0,2,1:T(8,128)(2,1)} %copy.79), channel_id=1, source_target_pairs={{0,4},{4,8},{8,12},{12,16},{16,20},{20,24},{24,28},{28,32},{32,36}... | collective-permute-start | bytes 393224 | tf_op jit(solution)/shard_map/ppermute | solution.py:12
  191.2 3.7 %fusion.85 = bf16[256,2,4,128]{0,3,2,1:T(8,128)(2,1)} fusion(f32[256,2,4,128]{0,3,2,1:T(8,128)S(1)} %copy-done.6, f32[256,2,4,128]{0,3,2,1:T(8,128)S(1)} %copy-done.5, f32[256,2,4,128]{0,3,2,1:T(8,128)S(1)} %copy-done.4, f32[256,2,4,128]{0,3,2,1:T(8,128)S(1)} %convolution_bitcast_fusion.3, f32[256,2,4,128]{0,3,2,1:T(8,128)S(1)} %copy-done.2, ...), kind=kOutput, calls=%fused_computation.138 | convolution fusion | flops 145489920 | bytes 19734528 | tf_op jit(solution)/shard_map/kgts,skd->kgtd/dot_general | solution.py:52
  195.0 29.0 %all-gather.2.cloned.1.call-done = bf16[1024,4096]{0,1:T(8,128)(2,1)} async-done(((bf16[1024,64]{0,1:T(8,128)(2,1)}), bf16[1024,4096]{0,1:T(8,128)(2,1)}) %all-gather.2.cloned.1.call-update) | async-done | bytes 8388624 | tf_op jit(solution)/shard_map/all_gather | solution.py:79
  224.0 6.0 %convolution_convert_fusion = bf16[256,4096]{1,0:T(8,128)(2,1)S(1)} fusion(bf16[256,1024]{0,1:T(8,128)(2,1)} %bitcast.758, bf16[1024,4096]{0,1:T(8,128)(2,1)} %all-gather.2.cloned.1.call-done), kind=kOutput, calls=%fused_computation | convolution fusion | flops 2148532224 | bytes 11010048 | tf_op jit(solution)/shard_map/dot_general | solution.py:77
  230.2 30.9 %all_to_all.5 = bf16[4,256,1024]{2,1,0:T(8,128)(2,1)S(1)} all-to-all(bf16[4,256,1024]{2,1,0:T(8,128)(2,1)S(1)} %bitcast.756), channel_id=1, replica_groups=mesh['seq'=64,'head'=4] {'head'}, dimensions={0} | all-to-all | bytes 4194304 | tf_op jit(solution)/shard_map/all_to_all | solution.py:22
  (251 shorter events, 68.0 us)
Async XLA Ops:
  6.5 217.5 %all-gather.2.cloned.1.call-start = ((), (), s32[]{:S(2)}) async-start(), calls=%async_computation.1 | async-start | bytes 8519680 | tf_op jit(solution)/shard_map/all_gather | solution.py:79
  7.5 30.2 %collective-permute-start.18 = (bf16[256,2,128]{2,0,1:T(8,128)(2,1)S(1)}, bf16[256,2,128]{2,0,1:T(8,128)(2,1)S(1)}, u32[]{:S(2)}, u32[]{:S(2)}) collective-permute-start(bf16[256,2,128]{2,0,1:T(8,128)(2,1)S(1)} %copy.77), channel_id=1, source_target_pairs={{0,40},{4,44},{8,48},{12,52},{16,56},{20,60},{24,64},{28,68},{32,7... | collective-permute-start | bytes 393224 | tf_op jit(solution)/shard_map/ppermute | solution.py:12
  14.5 29.3 %collective-permute-start.16 = (bf16[256,2,128]{2,0,1:T(8,128)(2,1)S(1)}, bf16[256,2,128]{2,0,1:T(8,128)(2,1)S(1)}, u32[]{:S(2)}, u32[]{:S(2)}) collective-permute-start(bf16[256,2,128]{2,0,1:T(8,128)(2,1)S(1)} %copy.77), channel_id=1, source_target_pairs={{0,36},{4,40},{8,44},{12,48},{16,52},{20,56},{24,60},{28,64},{32,6... | collective-permute-start | bytes 393224 | tf_op jit(solution)/shard_map/ppermute | solution.py:12
  18.2 28.7 %collective-permute-start.14 = (bf16[256,2,128]{2,0,1:T(8,128)(2,1)S(1)}, bf16[256,2,128]{2,0,1:T(8,128)(2,1)S(1)}, u32[]{:S(2)}, u32[]{:S(2)}) collective-permute-start(bf16[256,2,128]{2,0,1:T(8,128)(2,1)S(1)} %copy.77), channel_id=1, source_target_pairs={{0,32},{4,36},{8,40},{12,44},{16,48},{20,52},{24,56},{28,60},{32,6... | collective-permute-start | bytes 393224 | tf_op jit(solution)/shard_map/ppermute | solution.py:12
  21.8 29.7 %collective-permute-start.12 = (bf16[256,2,128]{2,0,1:T(8,128)(2,1)S(1)}, bf16[256,2,128]{2,0,1:T(8,128)(2,1)S(1)}, u32[]{:S(2)}, u32[]{:S(2)}) collective-permute-start(bf16[256,2,128]{2,0,1:T(8,128)(2,1)S(1)} %copy.77), channel_id=1, source_target_pairs={{0,28},{4,32},{8,36},{12,40},{16,44},{20,48},{24,52},{28,56},{32,6... | collective-permute-start | bytes 393224 | tf_op jit(solution)/shard_map/ppermute | solution.py:12
  30.9 24.2 %collective-permute-start.10 = (bf16[256,2,128]{2,0,1:T(8,128)(2,1)S(1)}, bf16[256,2,128]{2,0,1:T(8,128)(2,1)S(1)}, u32[]{:S(2)}, u32[]{:S(2)}) collective-permute-start(bf16[256,2,128]{2,0,1:T(8,128)(2,1)S(1)} %copy.77), channel_id=1, source_target_pairs={{0,24},{4,28},{8,32},{12,36},{16,40},{20,44},{24,48},{28,52},{32,5... | collective-permute-start | bytes 393224 | tf_op jit(solution)/shard_map/ppermute | solution.py:12
  37.8 21.9 %collective-permute-start.8 = (bf16[256,2,128]{2,0,1:T(8,128)(2,1)S(1)}, bf16[256,2,128]{2,0,1:T(8,128)(2,1)S(1)}, u32[]{:S(2)}, u32[]{:S(2)}) collective-permute-start(bf16[256,2,128]{2,0,1:T(8,128)(2,1)S(1)} %copy.77), channel_id=1, source_target_pairs={{0,20},{4,24},{8,28},{12,32},{16,36},{20,40},{24,44},{28,48},{32,5... | collective-permute-start | bytes 393224 | tf_op jit(solution)/shard_map/ppermute | solution.py:12
  43.8 18.9 %collective-permute-start.6 = (bf16[256,2,128]{2,0,1:T(8,128)(2,1)S(1)}, bf16[256,2,128]{2,0,1:T(8,128)(2,1)S(1)}, u32[]{:S(2)}, u32[]{:S(2)}) collective-permute-start(bf16[256,2,128]{2,0,1:T(8,128)(2,1)S(1)} %copy.77), channel_id=1, source_target_pairs={{0,16},{4,20},{8,24},{12,28},{16,32},{20,36},{24,40},{28,44},{32,4... | collective-permute-start | bytes 393224 | tf_op jit(solution)/shard_map/ppermute | solution.py:12
  68.7 25.8 %collective-permute-start.20 = (bf16[256,2,128]{2,0,1:T(8,128)(2,1)S(1)}, bf16[256,2,128]{2,0,1:T(8,128)(2,1)S(1)}, u32[]{:S(2)}, u32[]{:S(2)}) collective-permute-start(bf16[256,2,128]{2,0,1:T(8,128)(2,1)S(1)} %copy.77), channel_id=1, source_target_pairs={{0,44},{4,48},{8,52},{12,56},{16,60},{20,64},{24,68},{28,72},{32,7... | collective-permute-start | bytes 393224 | tf_op jit(solution)/shard_map/ppermute | solution.py:12
  70.6 26.6 %collective-permute-start.2 = (bf16[256,2,128]{2,0,1:T(8,128)(2,1)S(1)}, bf16[256,2,128]{2,0,1:T(8,128)(2,1)S(1)}, u32[]{:S(2)}, u32[]{:S(2)}) collective-permute-start(bf16[256,2,128]{2,0,1:T(8,128)(2,1)S(1)} %copy.77), channel_id=1, source_target_pairs={{0,8},{4,12},{8,16},{12,20},{16,24},{20,28},{24,32},{28,36},{32,40... | collective-permute-start | bytes 393224 | tf_op jit(solution)/shard_map/ppermute | solution.py:12
  75.4 23.6 %collective-permute-start = (bf16[256,2,128]{2,0,1:T(8,128)(2,1)S(1)}, bf16[256,2,128]{2,0,1:T(8,128)(2,1)S(1)}, u32[]{:S(2)}, u32[]{:S(2)}) collective-permute-start(bf16[256,2,128]{2,0,1:T(8,128)(2,1)S(1)} %copy.77), channel_id=1, source_target_pairs={{0,4},{4,8},{8,12},{12,16},{16,20},{20,24},{24,28},{28,32},{32,36}... | collective-permute-start | bytes 393224 | tf_op jit(solution)/shard_map/ppermute | solution.py:12
  77.4 31.4 %collective-permute-start.11 = (bf16[256,2,128]{0,2,1:T(8,128)(2,1)}, bf16[256,2,128]{0,2,1:T(8,128)(2,1)S(1)}, u32[]{:S(2)}, u32[]{:S(2)}) collective-permute-start(bf16[256,2,128]{0,2,1:T(8,128)(2,1)} %copy.79), channel_id=1, source_target_pairs={{0,24},{4,28},{8,32},{12,36},{16,40},{20,44},{24,48},{28,52},{32,5... | collective-permute-start | bytes 393224 | tf_op jit(solution)/shard_map/ppermute | solution.py:12
  83.7 28.8 %collective-permute-start.9 = (bf16[256,2,128]{0,2,1:T(8,128)(2,1)}, bf16[256,2,128]{0,2,1:T(8,128)(2,1)S(1)}, u32[]{:S(2)}, u32[]{:S(2)}) collective-permute-start(bf16[256,2,128]{0,2,1:T(8,128)(2,1)} %copy.79), channel_id=1, source_target_pairs={{0,20},{4,24},{8,28},{12,32},{16,36},{20,40},{24,44},{28,48},{32,5... | collective-permute-start | bytes 393224 | tf_op jit(solution)/shard_map/ppermute | solution.py:12
  94.5 22.3 %collective-permute-start.7 = (bf16[256,2,128]{0,2,1:T(8,128)(2,1)}, bf16[256,2,128]{0,2,1:T(8,128)(2,1)S(1)}, u32[]{:S(2)}, u32[]{:S(2)}) collective-permute-start(bf16[256,2,128]{0,2,1:T(8,128)(2,1)} %copy.79), channel_id=1, source_target_pairs={{0,16},{4,20},{8,24},{12,28},{16,32},{20,36},{24,40},{28,44},{32,4... | collective-permute-start | bytes 393224 | tf_op jit(solution)/shard_map/ppermute | solution.py:12
  97.2 27.6 %collective-permute-start.5 = (bf16[256,2,128]{0,2,1:T(8,128)(2,1)}, bf16[256,2,128]{0,2,1:T(8,128)(2,1)S(1)}, u32[]{:S(2)}, u32[]{:S(2)}) collective-permute-start(bf16[256,2,128]{0,2,1:T(8,128)(2,1)} %copy.79), channel_id=1, source_target_pairs={{0,12},{4,16},{8,20},{12,24},{16,28},{20,32},{24,36},{28,40},{32,4... | collective-permute-start | bytes 393224 | tf_op jit(solution)/shard_map/ppermute | solution.py:12
  99.0 27.8 %collective-permute-start.19 = (bf16[256,2,128]{0,2,1:T(8,128)(2,1)}, bf16[256,2,128]{0,2,1:T(8,128)(2,1)S(1)}, u32[]{:S(2)}, u32[]{:S(2)}) collective-permute-start(bf16[256,2,128]{0,2,1:T(8,128)(2,1)} %copy.79), channel_id=1, source_target_pairs={{0,40},{4,44},{8,48},{12,52},{16,56},{20,60},{24,64},{28,68},{32,7... | collective-permute-start | bytes 393224 | tf_op jit(solution)/shard_map/ppermute | solution.py:12
  108.8 21.6 %collective-permute-start.17 = (bf16[256,2,128]{0,2,1:T(8,128)(2,1)}, bf16[256,2,128]{0,2,1:T(8,128)(2,1)S(1)}, u32[]{:S(2)}, u32[]{:S(2)}) collective-permute-start(bf16[256,2,128]{0,2,1:T(8,128)(2,1)} %copy.79), channel_id=1, source_target_pairs={{0,36},{4,40},{8,44},{12,48},{16,52},{20,56},{24,60},{28,64},{32,6... | collective-permute-start | bytes 393224 | tf_op jit(solution)/shard_map/ppermute | solution.py:12
  112.6 19.9 %collective-permute-start.15 = (bf16[256,2,128]{0,2,1:T(8,128)(2,1)}, bf16[256,2,128]{0,2,1:T(8,128)(2,1)S(1)}, u32[]{:S(2)}, u32[]{:S(2)}) collective-permute-start(bf16[256,2,128]{0,2,1:T(8,128)(2,1)} %copy.79), channel_id=1, source_target_pairs={{0,32},{4,36},{8,40},{12,44},{16,48},{20,52},{24,56},{28,60},{32,6... | collective-permute-start | bytes 393224 | tf_op jit(solution)/shard_map/ppermute | solution.py:12
  126.9 32.1 %collective-permute-start.25 = (bf16[256,2,128]{0,2,1:T(8,128)(2,1)}, bf16[256,2,128]{0,2,1:T(8,128)(2,1)S(1)}, u32[]{:S(2)}, u32[]{:S(2)}) collective-permute-start(bf16[256,2,128]{0,2,1:T(8,128)(2,1)} %copy.79), channel_id=1, source_target_pairs={{0,52},{4,56},{8,60},{12,64},{16,68},{20,72},{24,76},{28,80},{32,8... | collective-permute-start | bytes 393224 | tf_op jit(solution)/shard_map/ppermute | solution.py:12
  130.4 30.6 %collective-permute-start.23 = (bf16[256,2,128]{0,2,1:T(8,128)(2,1)}, bf16[256,2,128]{0,2,1:T(8,128)(2,1)S(1)}, u32[]{:S(2)}, u32[]{:S(2)}) collective-permute-start(bf16[256,2,128]{0,2,1:T(8,128)(2,1)} %copy.79), channel_id=1, source_target_pairs={{0,48},{4,52},{8,56},{12,60},{16,64},{20,68},{24,72},{28,76},{32,8... | collective-permute-start | bytes 393224 | tf_op jit(solution)/shard_map/ppermute | solution.py:12
  132.5 36.0 %collective-permute-start.21 = (bf16[256,2,128]{0,2,1:T(8,128)(2,1)}, bf16[256,2,128]{0,2,1:T(8,128)(2,1)S(1)}, u32[]{:S(2)}, u32[]{:S(2)}) collective-permute-start(bf16[256,2,128]{0,2,1:T(8,128)(2,1)} %copy.79), channel_id=1, source_target_pairs={{0,44},{4,48},{8,52},{12,56},{16,60},{20,64},{24,68},{28,72},{32,7... | collective-permute-start | bytes 393224 | tf_op jit(solution)/shard_map/ppermute | solution.py:12
  135.5 34.7 %collective-permute-start.27 = (bf16[256,2,128]{0,2,1:T(8,128)(2,1)}, bf16[256,2,128]{0,2,1:T(8,128)(2,1)S(1)}, u32[]{:S(2)}, u32[]{:S(2)}) collective-permute-start(bf16[256,2,128]{0,2,1:T(8,128)(2,1)} %copy.79), channel_id=1, source_target_pairs={{0,56},{4,60},{8,64},{12,68},{16,72},{20,76},{24,80},{28,84},{32,8... | collective-permute-start | bytes 393224 | tf_op jit(solution)/shard_map/ppermute | solution.py:12
  140.5 32.5 %collective-permute-start.29 = (bf16[256,2,128]{0,2,1:T(8,128)(2,1)}, bf16[256,2,128]{0,2,1:T(8,128)(2,1)S(1)}, u32[]{:S(2)}, u32[]{:S(2)}) collective-permute-start(bf16[256,2,128]{0,2,1:T(8,128)(2,1)} %copy.79), channel_id=1, source_target_pairs={{0,60},{4,64},{8,68},{12,72},{16,76},{20,80},{24,84},{28,88},{32,9... | collective-permute-start | bytes 393224 | tf_op jit(solution)/shard_map/ppermute | solution.py:12
  161.1 29.4 %collective-permute-start.1 = (bf16[256,2,128]{0,2,1:T(8,128)(2,1)}, bf16[256,2,128]{0,2,1:T(8,128)(2,1)}, u32[]{:S(2)}, u32[]{:S(2)}) collective-permute-start(bf16[256,2,128]{0,2,1:T(8,128)(2,1)} %copy.79), channel_id=1, source_target_pairs={{0,4},{4,8},{8,12},{12,16},{16,20},{20,24},{24,28},{28,32},{32,36}... | collective-permute-start | bytes 393224 | tf_op jit(solution)/shard_map/ppermute | solution.py:12
  (69 other events, 1568.9 us)
Sparse Core Ops, SparseCore 0:
  32.4 191.6 all-gather.1
where the time goes:
time: 272 us; the launch traced here: 269 us
  starting transfers between devices  137 us (50%)
  matrix products  36.3 us (13%)
  blocking collectives  30.9 us (11%)
  waiting for transfers between devices  29.1 us (11%)
  other arithmetic  16.8 us (6%)
  between operations  15.1 us (6%)
  local copies, waits for them, and re-layouts  3.82 us (1%)
    ppermute x32, starting transfers between devices, from_behind(): return lax.ppermute(shard, axis, pairs)  137 us
    all_to_all x1, blocking collectives, sent_and_summed(): lax.all_to_all(in_blocks(shard, dim, devices), axis, 0, 0, tiled=True)  30.9 us
    all_gather x1, waiting for transfers between devices, body(): lax.all_gather(out_weight, 'seq', axis=1, tiled=True)  29 us
    dot_general x17, matrix products, absorb(): jnp.einsum('kgts,skd->kgtd', weights.astype(jnp.bfloat16), block_values,...  21 us
    reduce_sum x9, other arithmetic, absorb(): running_sum = running_sum * rescale + jnp.sum(weights, axis=-1)  12.1 us
    dot_general x17, matrix products, absorb(): jnp.einsum('tkgd,skd->kgts', grouped, block_keys, preferred_element_type=...  9.33 us
    dot_general x1, matrix products, body(): jnp.dot(attended, lax.all_gather(out_weight, 'seq', axis=1, tiled=True),...  5.96 us
  transfers between devices with their start and end apart: 33, of which 1 were waited for; matrix products, arithmetic and copies ran while one was open for 18% of the time, Pallas kernels for 0%

commit v1 on v0

v1 whole, which is shorter than its diff:
```python
import functools

import jax
import jax.numpy as jnp
from jax import lax
from jax.experimental import pallas as pl
from jax.experimental.pallas import tpu as pltpu
from jax.sharding import PartitionSpec as P

MESH = pl.DeviceIdType.MESH
NT = (((1,), (1,)), ((), ()))
BIG = 1e30
LOG2E = 1.4426950408889634
HS = 128
SH = 256
CH = 512
ROWS = 128
BF = jnp.bfloat16
F32 = jnp.float32


def kernel(
    q_in,
    kv_in,
    w_in,
    out,
    qb,
    own,
    oth,
    wb,
    mx,
    acc,
    ab,
    pf,
    pa,
    pr,
    rb,
    ss_kv, rs_kv, ss_q, rs_q,
    ss_z, rs_z, ss_x, rs_x,
    ss_c, rs_c,
    ss_w, rs_w,
    ss_wc, rs_wc,
    ss_a, rs_a,
    ss_p, rs_p,
    ss_o, rs_o,
):
    seq = lax.axis_index("seq")
    head = lax.axis_index("head")
    z, xh, y = seq // 8, (seq // 4) % 2, seq % 4
    xl, c = head // 2, head % 2

    def dev(zz, xx, yy, ll, cc):
        return (zz * 8 + xx * 4 + yy, ll * 2 + cc)

    zp, zm = lax.rem(z + 1, 8), lax.rem(z + 7, 8)
    d_zp = dev(zp, xh, y, xl, c)
    d_zm = dev(zm, xh, y, xl, c)
    d_x = dev(z, 1 - xh, y, xl, c)
    d_c = dev(z, xh, y, xl, 1 - c)
    d_l = dev(z, xh, y, 1 - xl, c)

    def remote(src, dst, ss, rs, device):
        return pltpu.make_async_remote_copy(
            src_ref=src, dst_ref=dst, send_sem=ss, recv_sem=rs,
            device_id=device, device_id_type=MESH,
        )

    barrier = pltpu.get_barrier_semaphore()
    for dy in range(4):
        for dc in range(2):
            if dy or dc:
                pl.semaphore_signal(
                    barrier, inc=1, device_id_type=MESH,
                    device_id=dev(z, xh, lax.rem(y + dy, 4), xl, lax.rem(c + dc, 2)),
                )
    for d in (d_zp, d_zm, d_x, d_l):
        pl.semaphore_signal(barrier, inc=1, device_id=d, device_id_type=MESH)
    pl.semaphore_wait(barrier, 11)

    jy = y % 2

    def to_head(i):
        dest = dev(z, xh, 2 * c + i, xl, y // 2)
        kv = remote(kv_in.at[i], own.at[0, :, pl.ds(jy * SH, SH), :], ss_kv.at[i], rs_kv.at[jy], dest)
        q = remote(q_in.at[i], qb.at[jy], ss_q.at[i], rs_q.at[jy], dest)
        return kv, q

    mine_here = c == y // 2

    def is_remote(i):
        return jnp.logical_not(jnp.logical_and(mine_here, jy == i))

    for i in range(2):
        @pl.when(is_remote(i))
        def _():
            to_head(i)[0].start()

    w_x = remote(w_in, wb.at[c, z, xh], ss_w.at[0], rs_w.at[0], d_x)
    w_x.start()
    for i in range(2):
        @pl.when(is_remote(i))
        def _():
            to_head(i)[1].start()

        @pl.when(jnp.logical_not(is_remote(i)))
        def _():
            own[0, :, i * SH : (i + 1) * SH, :] = kv_in[i]
            qb[i] = q_in[i]

    wb[c, z, xh] = w_in[...]

    def wait_in(which):
        for j in range(2):
            @pl.when(jnp.logical_not(jnp.logical_and(mine_here, jy == j)))
            def _():
                if which == 0:
                    remote(kv_in.at[0], own.at[0, :, pl.ds(j * SH, SH), :], ss_kv.at[0], rs_kv.at[j], d_c).wait_recv()
                else:
                    remote(q_in.at[0], qb.at[j], ss_q.at[0], rs_q.at[j], d_c).wait_recv()

    def w_up(s):
        b = wb.at[c, lax.rem(z + 8 - s, 8)]
        return remote(b, b, ss_w.at[1 + s], rs_w.at[1 + s], d_zp)

    def w_down(s):
        b = wb.at[c, lax.rem(z + s, 8)]
        return remote(b, b, ss_w.at[4 + s], rs_w.at[4 + s], d_zm)

    def w_core(k, block):
        b = wb.at[c, block]
        return remote(b, b, ss_wc.at[k], rs_wc.at[k], d_c)

    def w_up_got(s):
        w_up(s).wait_recv()
        if s < 2:
            w_up(s + 1).start()
        w_core(1 + s, lax.rem(z + 7 - s, 8)).start()

    def w_down_got(s):
        w_down(s).wait_recv()
        if s < 3:
            w_down(s + 1).start()
        w_core(4 + s, lax.rem(z + 1 + s, 8)).start()

    z_send = [
        remote(own.at[0], own.at[2], ss_z.at[0], rs_z.at[0], d_zp),
        remote(own.at[2], own.at[4], ss_z.at[1], rs_z.at[1], d_zp),
    ]

    def x_send(item, k):
        return remote(own.at[item], own.at[1 + 2 * k], ss_x.at[k], rs_x.at[k], d_x)

    def c_send(item, k):
        return remote(own.at[item], oth.at[k], ss_c.at[k], rs_c.at[k], d_c)

    wait_in(0)
    z_send[0].start()

    @pl.when(xh == 0)
    def _():
        x_send(0, 0).start()

    @pl.when(c == 0)
    def _():
        c_send(0, 0).start()

    w_x.wait_recv()
    w_core(0, z).start()
    w_up(0).start()
    w_down(0).start()
    wait_in(1)

    hg = 4 * z + 2 * xh + c
    scale = LOG2E / HS**0.5

    def bias(delta):
        return jnp.where(hg >= delta, 0.0, BIG).astype(F32)

    ones = jnp.ones((CH, HS), BF)

    def attend(j, segs, first=False):
        for g in range(4):
            for h in range(SH // ROWS):
                rows = slice(h * ROWS, (h + 1) * ROWS)
                q = qb[j, g, rows, :]
                scores, tops = [], []
                for ref, lo, size, mask, b in segs:
                    s = lax.dot_general(q, ref[0, lo : lo + size, :], NT, preferred_element_type=F32)
                    if mask is not None:
                        t = lax.broadcasted_iota(jnp.int32, s.shape, 0) + h * ROWS
                        k = lax.broadcasted_iota(jnp.int32, s.shape, 1)
                        s = jnp.where(k <= t if mask == "upto" else k > t, s, -BIG)
                    m = jnp.max(s, axis=1, keepdims=True)
                    scores.append(s)
                    tops.append(m if b is None else m - b)
                top = tops[0]
                for m in tops[1:]:
                    top = jnp.maximum(top, m)
                if first:
                    new = jnp.broadcast_to(top, (ROWS, HS))
                else:
                    old = mx[j, g, rows, :]
                    new = jnp.maximum(old, top)
                total = None
                for s, (ref, lo, size, mask, b) in zip(scores, segs):
                    m = new[:, :1] if b is None else new[:, :1] + b
                    p = jnp.exp2((s - m) * scale).astype(BF)
                    v = jnp.concatenate([ref[1, lo : lo + size, :], ones[:size]], 1)
                    u = jnp.dot(p, v, preferred_element_type=F32)
                    total = u if total is None else total + u
                if first:
                    acc[j, g, rows, :] = total
                else:
                    a = jnp.exp2((old - new) * scale)
                    acc[j, g, rows, :] = acc[j, g, rows, :] * jnp.concatenate([a, a], 1) + total
                mx[j, g, rows, :] = new

    def diagonal(j):
        last = (own.at[0], j * SH, SH, "upto", None)
        return [(own.at[0], 0, SH, None, None), last] if j else [last]

    def far(j):
        edge = (own.at[4], j * SH, SH, "after", bias(8))
        return [edge] if j else [edge, (own.at[4], SH, SH, None, bias(8))]

    def full(ref, delta):
        return (ref, 0, CH, None, bias(delta))

    odd = [jnp.where(c == 0, p, q) for p, q in ((3, 1), (1, 5), (7, 3), (5, 7))]

    z_send[0].wait_recv()
    z_send[1].start()

    @pl.when(xh == 0)
    def _():
        x_send(2, 1).start()

    @pl.when(xh == 1)
    def _():
        x_send(2, 0).start()

    @pl.when(c == 0)
    def _():
        c_send(2, 1).start()

    @pl.when(c == 1)
    def _():
        c_send(2, 0).start()

    for j in range(2):
        attend(j, diagonal(j) + [full(own.at[2], 4)], first=True)
    w_up_got(0)
    w_down_got(0)

    x_send(0, 0).wait_recv()

    @pl.when(c == 0)
    def _():
        c_send(1, 2).start()

    @pl.when(c == 1)
    def _():
        c_send(1, 1).start()

    c_send(0, 0).wait_recv()
    for j in range(2):
        attend(j, [full(own.at[1], 2), full(oth.at[0], odd[0])])

    z_send[1].wait_recv()

    @pl.when(xh == 1)
    def _():
        x_send(4, 1).start()

    @pl.when(c == 1)
    def _():
        c_send(4, 2).start()

    w_up_got(1)
    w_down_got(1)
    c_send(0, 1).wait_recv()
    c_send(0, 2).wait_recv()

    attend(0, far(0) + [full(oth.at[1], odd[1]), full(oth.at[2], odd[2])])

    x_send(0, 1).wait_recv()
    c_send(3, 3).start()
    c_send(0, 3).wait_recv()
    w_up_got(2)
    w_down_got(2)

    def a_send(j, k):
        b = ab.at[y, j]
        return remote(b, b, ss_a.at[k, j], rs_a.at[k, j], dev(z, xh, lax.rem(y + k + 1, 4), xl, c))

    def finish(j):
        attend(j, [full(own.at[3], 6), full(oth.at[3], odd[3])])
        for g in range(4):
            a = acc[j, g]
            ab[y, j, :, g * HS : (g + 1) * HS] = (a[:, :HS] / a[:, HS:]).astype(BF)
        for k in range(3):
            a_send(j, k).start()

    finish(0)
    attend(1, far(1) + [full(oth.at[1], odd[1]), full(oth.at[2], odd[2])])
    finish(1)
    w_down_got(3)
    for k in range(8):
        w_core(k, z).wait_recv()

    def partial(j, half, i):
        total = None
        zz = half * 4 + i * 2
        for yy in range(4):
            w = wb[yy // 2, pl.ds(zz, 2), :, :, (yy % 2) * CH : (yy % 2 + 1) * CH].reshape(SH, CH)
            u = lax.dot_general(ab[yy, j], w, NT, preferred_element_type=F32)
            total = u if total is None else total + u
        return total

    def p_send(j, i):
        return remote(pa.at[j, i], pr.at[j, i], ss_p.at[j, i], rs_p.at[j, i], d_l)

    def o_send(j, i):
        return remote(rb.at[j, i], out.at[y], ss_o.at[j, i], rs_o.at[y], dev(z, xh, 2 * c + j, xl, i))

    def o_here(j, i):
        return jnp.logical_and(y == 2 * c + j, c == i)

    for j in range(2):
        for k in range(3):
            a_send(j, k).wait_recv()
        for i in range(2):
            pa[j, i] = partial(j, 1 - xl, i).astype(BF)
            p_send(j, i).start()
        for i in range(2):
            pf[j, i] = partial(j, xl, i)
    for j in range(2):
        for i in range(2):
            p_send(j, i).wait_recv()
            total = (pf[j, i] + pr[j, i].astype(F32)).astype(BF)

            @pl.when(o_here(j, i))
            def _():
                out[y] = total

            @pl.when(jnp.logical_not(o_here(j, i)))
            def _():
                rb[j, i] = total
                o_send(j, i).start()

    for yy in range(4):
        @pl.when(jnp.logical_not(jnp.logical_and(yy == y, c == y // 2)))
        def _():
            remote(rb.at[0, 0], out.at[yy], ss_o.at[0, 0], rs_o.at[yy], d_c).wait_recv()
    for i in range(2):
        @pl.when(is_remote(i))
        def _():
            for copy in to_head(i):
                copy.wait_send()
    w_x.wait_send()
    for s in range(3):
        w_up(s).wait_send()
    for s in range(4):
        w_down(s).wait_send()
    for k in range(8):
        w_core(k, z).wait_send()
    for k in range(2):
        z_send[k].wait_send()
        x_send(0, k).wait_send()
    for k in range(4):
        c_send(0, k).wait_send()
    for j in range(2):
        for k in range(3):
            a_send(j, k).wait_send()
        for i in range(2):
            p_send(j, i).wait_send()

            @pl.when(jnp.logical_not(o_here(j, i)))
            def _():
                o_send(j, i).wait_send()


def body(queries, keys, values, out_weight):
    tokens = queries.shape[0]
    q = queries.reshape(tokens, 2, 4, HS).transpose(1, 2, 0, 3)
    kv = jnp.stack([keys, values]).transpose(2, 0, 1, 3)
    dma = pltpu.SemaphoreType.DMA
    sems = [dma((2,))] * 8 + [dma((4,))] * 2 + [dma((8,))] * 4 + [dma((3, 2))] * 2 + [dma((2, 2))] * 3 + [dma((4,))]
    vmem = pl.BlockSpec(memory_space=pltpu.VMEM)
    r = pl.pallas_call(
        kernel,
        name="layer",
        out_shape=jax.ShapeDtypeStruct((4, SH, SH), BF),
        in_specs=[vmem] * 3,
        out_specs=vmem,
        scratch_shapes=[
            pltpu.VMEM((2, 4, SH, HS), BF),
            pltpu.VMEM((5, 2, CH, HS), BF),
            pltpu.VMEM((4, 2, CH, HS), BF),
            pltpu.VMEM((2, 8, 2, 64, 1024), BF),
            pltpu.VMEM((2, 4, SH, HS), F32),
            pltpu.VMEM((2, 4, SH, 2 * HS), F32),
            pltpu.VMEM((4, 2, SH, CH), BF),
            pltpu.VMEM((2, 2, SH, SH), F32),
            pltpu.VMEM((2, 2, SH, SH), BF),
            pltpu.VMEM((2, 2, SH, SH), BF),
            pltpu.VMEM((2, 2, SH, SH), BF),
            *sems,
        ],
        compiler_params=pltpu.CompilerParams(
            collective_id=0, has_side_effects=True, vmem_limit_bytes=48 * 2**20
        ),
    )(q, kv, out_weight.T)
    return r.reshape(4, tokens, 4, 64).transpose(1, 2, 0, 3).reshape(tokens, 1024)


def solution(mesh):
    return jax.shard_map(
        body,
        mesh=mesh,
        in_specs=(
            P("seq", "head", None),
            P("seq", "head", None),
            P("seq", "head", None),
            P("head", "seq"),
        ),
        out_specs=P("seq", "head"),
        check_vma=False,
    )
```

time: 272 us -> 91.4 us (0.34)
  the two profiles are of different devices: /device:TPU:1 before, /device:TPU:9 now
where the time goes in v1:
time: 91.4 us; the launch traced here: 91.3 us
  Pallas kernels  87.9 us (96%)
  local copies, waits for them, and re-layouts  3.28 us (4%)
    pallas_call x1, Pallas kernels, body(): pl.pallas_call(kernel, name='layer', out_shape=jax.ShapeDtypeStruct((4, S...  87.9 us

profile of v1, /device:TPU:9, one launch (start us, length us, event | category | flops | bytes accessed | tf_op | source)
XLA Modules:
  0.0 91.3 jit_solution(15280639910886741179)
XLA Ops:
  0.0 0.0 copy-start.1
  0.0 1.1 %copy_bitcast_fusion = (bf16[1,256,2,128]{3,1,0,2:T(8,128)(2,1)S(1)}, bf16[1,256,2,128]{3,1,0,2:T(8,128)(2,1)S(1)}) fusion(bf16[256,2,128]{2,1,0:T(2,128)(2,1)} %param.6, bf16[256,2,128]{2,1,0:T(2,128)(2,1)} %param.5), kind=kLoop, calls=%fused_computation.1 | loop fusion | bytes 524288 | tf_op jit(solution)/shard_map/stack | solution.py:386
  1.1 0.1 copy-done.1
  1.2 0.0 copy-start
  1.2 0.1 copy.9
  1.2 0.8 copy-done
  2.1 87.9 %layer.1 = bf16[4,256,256]{2,1,0:T(8,128)(2,1)S(1)} custom-call(bf16[2,4,256,128]{3,2,1,0:T(8,128)(2,1)S(1)} %bitcast.14, bf16[2,2,256,128]{3,2,1,0:T(8,128)(2,1)S(1)} %maximum_bitcast_fusion.kv_in, bf16[64,1024]{1,0:T(8,128)(2,1)S(1)} %bitcast.15), custom_call_target="tpu_custom_call" | custom-call | tf_op jit(solution)/shard_map/layer/pallas_call | solution.py:390
  90.0 0.2 copy.12
  90.3 1.0 %copy.14 = bf16[256,1024]{1,0:T(8,128)(2,1)} copy(bf16[256,1024]{0,1:T(8,128)(2,1)S(1)} %bitcast.17) | data formatting | bytes 1048576 | tf_op jit(solution)/shard_map/reshape | solution.py:414
  (2 shorter events, 0.1 us)
Async XLA Ops:
  0.0 1.2 %copy-start.1 = (bf16[256,8,128]{2,1,0:T(8,128)(2,1)S(1)}, bf16[256,8,128]{2,1,0:T(8,128)(2,1)}, u32[]{:S(2)}) copy-start(bf16[256,8,128]{2,1,0:T(8,128)(2,1)} %param.4) | copy-start | bytes 1572868
  1.2 0.9 copy-start

commit v2 on v1

--- a/solution.py
+++ b/solution.py
@@ -15,6 +15,7 @@
 SH = 256
 CH = 512
 ROWS = 128
+DOWN, UP = 5, 2
 BF = jnp.bfloat16
 F32 = jnp.float32
 
@@ -38,9 +39,11 @@
     ss_kv, rs_kv, ss_q, rs_q,
     ss_z, rs_z, ss_x, rs_x,
     ss_c, rs_c,
+    ss_wx, rs_wx,
     ss_w, rs_w,
     ss_wc, rs_wc,
     ss_a, rs_a,
+    ss_r, rs_r,
     ss_p, rs_p,
     ss_o, rs_o,
 ):
@@ -95,7 +98,7 @@
         def _():
             to_head(i)[0].start()
 
-    w_x = remote(w_in, wb.at[c, z, xh], ss_w.at[0], rs_w.at[0], d_x)
+    w_x = remote(w_in, wb.at[c, z, xh], ss_wx.at[0], rs_wx.at[0], d_x)
     w_x.start()
     for i in range(2):
         @pl.when(is_remote(i))
@@ -109,66 +112,87 @@
 
     wb[c, z, xh] = w_in[...]
 
-    def wait_in(which):
-        for j in range(2):
-            @pl.when(jnp.logical_not(jnp.logical_and(mine_here, jy == j)))
-            def _():
-                if which == 0:
-                    remote(kv_in.at[0], own.at[0, :, pl.ds(j * SH, SH), :], ss_kv.at[0], rs_kv.at[j], d_c).wait_recv()
-                else:
-                    remote(q_in.at[0], qb.at[j], ss_q.at[0], rs_q.at[j], d_c).wait_recv()
-
-    def w_up(s):
-        b = wb.at[c, lax.rem(z + 8 - s, 8)]
-        return remote(b, b, ss_w.at[1 + s], rs_w.at[1 + s], d_zp)
-
-    def w_down(s):
-        b = wb.at[c, lax.rem(z + s, 8)]
-        return remote(b, b, ss_w.at[4 + s], rs_w.at[4 + s], d_zm)
-
-    def w_core(k, block):
+    def wait_in(which, j):
+        @pl.when(jnp.logical_not(jnp.logical_and(mine_here, jy == j)))
+        def _():
+            if which == 0:
+                remote(kv_in.at[0], half(0, j), ss_kv.at[0], rs_kv.at[j], d_c).wait_recv()
+            else:
+                remote(q_in.at[0], qb.at[j], ss_q.at[0], rs_q.at[j], d_c).wait_recv()
+
+    def w_ring(k, s, h):
+        b = wb.at[c, lax.rem(z + s, 8) if k == 0 else lax.rem(z + 8 - s, 8), h]
+        n = s if k == 0 else DOWN + s
+        return remote(b, b, ss_w.at[n, h], rs_w.at[n, h], d_zp if k else d_zm)
+
+    def w_core(n, block):
         b = wb.at[c, block]
-        return remote(b, b, ss_wc.at[k], rs_wc.at[k], d_c)
-
-    def w_up_got(s):
-        w_up(s).wait_recv()
-        if s < 2:
-            w_up(s + 1).start()
-        w_core(1 + s, lax.rem(z + 7 - s, 8)).start()
-
-    def w_down_got(s):
-        w_down(s).wait_recv()
-        if s < 3:
-            w_down(s + 1).start()
-        w_core(4 + s, lax.rem(z + 1 + s, 8)).start()
-
-    z_send = [
-        remote(own.at[0], own.at[2], ss_z.at[0], rs_z.at[0], d_zp),
-        remote(own.at[2], own.at[4], ss_z.at[1], rs_z.at[1], d_zp),
-    ]
-
-    def x_send(item, k):
-        return remote(own.at[item], own.at[1 + 2 * k], ss_x.at[k], rs_x.at[k], d_x)
-
-    def c_send(item, k):
-        return remote(own.at[item], oth.at[k], ss_c.at[k], rs_c.at[k], d_c)
-
-    wait_in(0)
-    z_send[0].start()
-
-    @pl.when(xh == 0)
-    def _():
-        x_send(0, 0).start()
-
-    @pl.when(c == 0)
-    def _():
-        c_send(0, 0).start()
-
+        return remote(b, b, ss_wc.at[n], rs_wc.at[n], d_c)
+
+    def w_got(k, s):
+        for h in range(2):
+            w_ring(k, s, h).wait_recv()
+            if s + 1 < (UP if k else DOWN):
+                w_ring(k, s + 1, h).start()
+        if k == 0:
+            w_core(1 + s, lax.rem(z + 1 + s, 8)).start()
+        else:
+            w_core(1 + DOWN + s, lax.rem(z + 7 - s, 8)).start()
+
+    def half(item, h):
+        return own.at[item, :, pl.ds(h * SH, SH), :]
+
+    def z_send(k, h):
+        return remote(half(2 * k, h), half(2 * k + 2, h), ss_z.at[k, h], rs_z.at[k, h], d_zp)
+
+    def x_send(item, k, h):
+        return remote(half(item, h), half(1 + 2 * k, h), ss_x.at[k, h], rs_x.at[k, h], d_x)
+
+    def c_send(item, k, h):
+        return remote(half(item, h), oth.at[k, :, pl.ds(h * SH, SH), :], ss_c.at[k, h], rs_c.at[k, h], d_c)
+
+    def start_if(condition, make, *args):
+        @pl.when(condition)
+        def _():
+            make(*args).start()
+
+    for h in range(2):
+        wait_in(0, h)
+        z_send(0, h).start()
+        start_if(xh == 0, x_send, 0, 0, h)
+        start_if(c == 0, c_send, 0, 0, h)
     w_x.wait_recv()
+    for h in range(2):
+        w_ring(0, 0, h).start()
     w_core(0, z).start()
-    w_up(0).start()
-    w_down(0).start()
-    wait_in(1)
+    for j in range(2):
+        wait_in(1, j)
+
+    def got_z1(h):
+        z_send(0, h).wait_recv()
+        z_send(1, h).start()
+        start_if(xh == 0, x_send, 2, 1, h)
+        start_if(xh == 1, x_send, 2, 0, h)
+        start_if(c == 0, c_send, 2, 1, h)
+        start_if(c == 1, c_send, 2, 0, h)
+
+    def got_a(h):
+        x_send(0, 0, h).wait_recv()
+        start_if(c == 0, c_send, 1, 2, h)
+        start_if(c == 1, c_send, 1, 1, h)
+
+    def got_z2(h):
+        z_send(1, h).wait_recv()
+        start_if(xh == 1, x_send, 4, 1, h)
+        start_if(c == 1, c_send, 4, 2, h)
+
+    def got_b(h):
+        x_send(0, 1, h).wait_recv()
+        c_send(3, 3, h).start()
+
+    def got_c(k):
+        for h in range(2):
+            c_send(0, k, h).wait_recv()
 
     hg = 4 * z + 2 * xh + c
     scale = LOG2E / HS**0.5
@@ -228,83 +252,62 @@
 
     odd = [jnp.where(c == 0, p, q) for p, q in ((3, 1), (1, 5), (7, 3), (5, 7))]
 
-    z_send[0].wait_recv()
-    z_send[1].start()
-
-    @pl.when(xh == 0)
-    def _():
-        x_send(2, 1).start()
-
-    @pl.when(xh == 1)
-    def _():
-        x_send(2, 0).start()
-
-    @pl.when(c == 0)
-    def _():
-        c_send(2, 1).start()
-
-    @pl.when(c == 1)
-    def _():
-        c_send(2, 0).start()
-
-    for j in range(2):
-        attend(j, diagonal(j) + [full(own.at[2], 4)], first=True)
-    w_up_got(0)
-    w_down_got(0)
-
-    x_send(0, 0).wait_recv()
-
-    @pl.when(c == 0)
-    def _():
-        c_send(1, 2).start()
-
-    @pl.when(c == 1)
-    def _():
-        c_send(1, 1).start()
-
-    c_send(0, 0).wait_recv()
-    for j in range(2):
-        attend(j, [full(own.at[1], 2), full(oth.at[0], odd[0])])
-
-    z_send[1].wait_recv()
-
-    @pl.when(xh == 1)
-    def _():
-        x_send(4, 1).start()
-
-    @pl.when(c == 1)
-    def _():
-        c_send(4, 2).start()
-
-    w_up_got(1)
-    w_down_got(1)
-    c_send(0, 1).wait_recv()
-    c_send(0, 2).wait_recv()
-
-    attend(0, far(0) + [full(oth.at[1], odd[1]), full(oth.at[2], odd[2])])
-
-    x_send(0, 1).wait_recv()
-    c_send(3, 3).start()
-    c_send(0, 3).wait_recv()
-    w_up_got(2)
-    w_down_got(2)
-
-    def a_send(j, k):
+    yp, ym = lax.rem(y + 1, 4), lax.rem(y + 3, 4)
+
+    def a_send(k, j):
         b = ab.at[y, j]
-        return remote(b, b, ss_a.at[k, j], rs_a.at[k, j], dev(z, xh, lax.rem(y + k + 1, 4), xl, c))
+        return remote(b, b, ss_a.at[k, j], rs_a.at[k, j], dev(z, xh, ym if k else yp, xl, c))
+
+    def a_relay(k, j):
+        b = ab.at[yp if k else ym, j, pl.ds(k * ROWS, ROWS), :]
+        return remote(b, b, ss_r.at[k, j], rs_r.at[k, j], dev(z, xh, ym if k else yp, xl, c))
+
+    def a_got(j):
+        for k in range(2):
+            a_send(k, j).wait_recv()
+            a_relay(k, j).start()
 
     def finish(j):
         attend(j, [full(own.at[3], 6), full(oth.at[3], odd[3])])
         for g in range(4):
             a = acc[j, g]
             ab[y, j, :, g * HS : (g + 1) * HS] = (a[:, :HS] / a[:, HS:]).astype(BF)
-        for k in range(3):
-            a_send(j, k).start()
-
+        for k in range(2):
+            a_send(k, j).start()
+
+    got_z1(0)
+    got_z1(1)
+    for h in range(2):
+        w_ring(1, 0, h).start()
+    attend(0, diagonal(0) + [full(own.at[2], 4)], first=True)
+    w_got(0, 0)
+    attend(1, diagonal(1) + [full(own.at[2], 4)], first=True)
+    got_a(0)
+    got_z2(0)
+    got_c(0)
+    for j in range(2):
+        attend(j, [full(oth.at[0], odd[0])])
+    got_a(1)
+    got_z2(1)
+    attend(0, [full(own.at[1], 2)] + far(0))
+    got_b(0)
+    got_c(1)
+    got_c(2)
+    attend(0, [full(oth.at[1], odd[1]), full(oth.at[2], odd[2])])
+    w_got(0, 1)
+    got_b(1)
+    attend(1, [full(own.at[1], 2)] + far(1))
+    got_c(3)
     finish(0)
-    attend(1, far(1) + [full(oth.at[1], odd[1]), full(oth.at[2], odd[2])])
+    attend(1, [full(oth.at[1], odd[1]), full(oth.at[2], odd[2])])
     finish(1)
-    w_down_got(3)
+    w_got(1, 0)
+    w_got(0, 2)
+    a_got(0)
+    w_got(1, 1)
+    w_got(0, 3)
+    a_got(1)
+    w_got(0, 4)
     for k in range(8):
         w_core(k, z).wait_recv()
 
@@ -327,8 +330,8 @@
         return jnp.logical_and(y == 2 * c + j, c == i)
 
     for j in range(2):
-        for k in range(3):
-            a_send(j, k).wait_recv()
+        for k in range(2):
+            a_relay(k, j).wait_recv()
         for i in range(2):
             pa[j, i] = partial(j, 1 - xl, i).astype(BF)
             p_send(j, i).start()
@@ -358,20 +361,20 @@
             for copy in to_head(i):
                 copy.wait_send()
     w_x.wait_send()
-    for s in range(3):
-        w_up(s).wait_send()
-    for s in range(4):
-        w_down(s).wait_send()
+    for h in range(2):
+        for k in range(2):
+            for n in range(UP if k else DOWN):
+                w_ring(k, n, h).wait_send()
+            z_send(k, h).wait_send()
+            x_send(0, k, h).wait_send()
+        for k in range(4):
+            c_send(0, k, h).wait_send()
     for k in range(8):
         w_core(k, z).wait_send()
-    for k in range(2):
-        z_send[k].wait_send()
-        x_send(0, k).wait_send()
-    for k in range(4):
-        c_send(0, k).wait_send()
     for j in range(2):
-        for k in range(3):
-            a_send(j, k).wait_send()
+        for k in range(2):
+            a_send(k, j).wait_send()
+            a_relay(k, j).wait_send()
         for i in range(2):
             p_send(j, i).wait_send()
 
@@ -385,7 +388,8 @@
     q = queries.reshape(tokens, 2, 4, HS).transpose(1, 2, 0, 3)
     kv = jnp.stack([keys, values]).transpose(2, 0, 1, 3)
     dma = pltpu.SemaphoreType.DMA
-    sems = [dma((2,))] * 8 + [dma((4,))] * 2 + [dma((8,))] * 4 + [dma((3, 2))] * 2 + [dma((2, 2))] * 3 + [dma((4,))]
+    shapes = [(2,)] * 4 + [(2, 2)] * 4 + [(4, 2)] * 2 + [(1,)] * 2 + [(DOWN + UP, 2)] * 2 + [(8,)] * 2 + [(2, 2)] * 7 + [(4,)]
+    sems = [dma(shape) for shape in shapes]
     vmem = pl.BlockSpec(memory_space=pltpu.VMEM)
     r = pl.pallas_call(
         kernel,

time: 91.4 us -> 78.6 us (0.86)
  the two profiles are of different devices: /device:TPU:9 before, /device:TPU:1 now
where the time goes in v2:
time: 78.6 us; the launch traced here: 78.5 us
  Pallas kernels  75.1 us (96%)
  local copies, waits for them, and re-layouts  3.28 us (4%)
    pallas_call x1, Pallas kernels, body(): pl.pallas_call(kernel, name='layer', out_shape=jax.ShapeDtypeStruct((4, S...  75.1 us

profile of v2, /device:TPU:1, one launch (start us, length us, event | category | flops | bytes accessed | tf_op | source)
XLA Modules:
  0.0 78.5 jit_solution(17777273619513912179)
XLA Ops:
  0.0 0.0 copy-start.1
  0.0 1.1 %copy_bitcast_fusion = (bf16[1,256,2,128]{3,1,0,2:T(8,128)(2,1)S(1)}, bf16[1,256,2,128]{3,1,0,2:T(8,128)(2,1)S(1)}) fusion(bf16[256,2,128]{2,1,0:T(2,128)(2,1)} %param.6, bf16[256,2,128]{2,1,0:T(2,128)(2,1)} %param.5), kind=kLoop, calls=%fused_computation.1 | loop fusion | bytes 524288 | tf_op jit(solution)/shard_map/stack | solution.py:389
  1.1 0.1 copy-done.1
  1.2 0.0 copy-start
  1.2 0.1 copy.9
  1.2 0.8 %copy-done = bf16[1024,64]{0,1:T(8,128)(2,1)S(1)} copy-done((bf16[1024,64]{0,1:T(8,128)(2,1)S(1)}, bf16[1024,64]{0,1:T(8,128)(2,1)}, u32[]{:S(2)}) %copy-start) | copy-done | bytes 131096
  2.1 75.1 %layer.1 = bf16[4,256,256]{2,1,0:T(8,128)(2,1)S(1)} custom-call(bf16[2,4,256,128]{3,2,1,0:T(8,128)(2,1)S(1)} %bitcast.14, bf16[2,2,256,128]{3,2,1,0:T(8,128)(2,1)S(1)} %maximum_bitcast_fusion.kv_in, bf16[64,1024]{1,0:T(8,128)(2,1)S(1)} %bitcast.15), custom_call_target="tpu_custom_call" | custom-call | tf_op jit(solution)/shard_map/layer/pallas_call | solution.py:394
  77.2 0.2 copy.12
  77.5 1.0 %copy.14 = bf16[256,1024]{1,0:T(8,128)(2,1)} copy(bf16[256,1024]{0,1:T(8,128)(2,1)S(1)} %bitcast.17) | data formatting | bytes 1048576 | tf_op jit(solution)/shard_map/reshape | solution.py:418
  (2 shorter events, 0.1 us)
Async XLA Ops:
  0.0 1.2 %copy-start.1 = (bf16[256,8,128]{2,1,0:T(8,128)(2,1)S(1)}, bf16[256,8,128]{2,1,0:T(8,128)(2,1)}, u32[]{:S(2)}) copy-start(bf16[256,8,128]{2,1,0:T(8,128)(2,1)} %param.4) | copy-start | bytes 1572868
  1.2 0.9 %copy-start = (bf16[1024,64]{0,1:T(8,128)(2,1)S(1)}, bf16[1024,64]{0,1:T(8,128)(2,1)}, u32[]{:S(2)}) copy-start(bf16[1024,64]{0,1:T(8,128)(2,1)} %param.7) | copy-start | bytes 393220

commit v3 on v2

--- a/solution.py
+++ b/solution.py
@@ -129,14 +129,13 @@
         b = wb.at[c, block]
         return remote(b, b, ss_wc.at[n], rs_wc.at[n], d_c)
 
-    def w_got(k, s):
-        for h in range(2):
-            w_ring(k, s, h).wait_recv()
-            if s + 1 < (UP if k else DOWN):
-                w_ring(k, s + 1, h).start()
-        if k == 0:
+    def w_got(k, s, h):
+        w_ring(k, s, h).wait_recv()
+        if s + 1 < (UP if k else DOWN):
+            w_ring(k, s + 1, h).start()
+        if h == 1 and k == 0:
             w_core(1 + s, lax.rem(z + 1 + s, 8)).start()
-        else:
+        if h == 1 and k == 1:
             w_core(1 + DOWN + s, lax.rem(z + 7 - s, 8)).start()
 
     def half(item, h):
@@ -254,107 +253,142 @@
 
     yp, ym = lax.rem(y + 1, 4), lax.rem(y + 3, 4)
 
-    def a_send(k, j):
-        b = ab.at[y, j]
-        return remote(b, b, ss_a.at[k, j], rs_a.at[k, j], dev(z, xh, ym if k else yp, xl, c))
-
-    def a_relay(k, j):
-        b = ab.at[yp if k else ym, j, pl.ds(k * ROWS, ROWS), :]
-        return remote(b, b, ss_r.at[k, j], rs_r.at[k, j], dev(z, xh, ym if k else yp, xl, c))
-
-    def a_got(j):
+    def a_send(k, t):
+        b = ab.at[y, t]
+        return remote(b, b, ss_a.at[k, t], rs_a.at[k, t], dev(z, xh, ym if k else yp, xl, c))
+
+    def a_relay(k, t):
+        b = ab.at[yp if k else ym, t, pl.ds(k * 64, 64), :]
+        return remote(b, b, ss_r.at[k, t], rs_r.at[k, t], dev(z, xh, ym if k else yp, xl, c))
+
+    def a_start(t):
         for k in range(2):
-            a_send(k, j).wait_recv()
-            a_relay(k, j).start()
+            a_send(k, t).start()
+
+    def a_got(t):
+        for k in range(2):
+            a_send(k, t).wait_recv()
+            a_relay(k, t).start()
+
+    def a_all(t):
+        for k in range(2):
+            a_relay(k, t).wait_recv()
 
     def finish(j):
         attend(j, [full(own.at[3], 6), full(oth.at[3], odd[3])])
-        for g in range(4):
-            a = acc[j, g]
-            ab[y, j, :, g * HS : (g + 1) * HS] = (a[:, :HS] / a[:, HS:]).astype(BF)
-        for k in range(2):
-            a_send(k, j).start()
+        for h in range(2):
+            rows = slice(h * ROWS, (h + 1) * ROWS)
+            for g in range(4):
+                a = acc[j, g, rows, :]
+                ab[y, 2 * j + h, :, g * HS : (g + 1) * HS] = (a[:, :HS] / a[:, HS:]).astype(BF)
+
+    def partial(t, side):
+        total = None
+        for yy in range(4):
+            w = wb[yy // 2, pl.ds(side * 4, 4), :, :, (yy % 2) * CH : (yy % 2 + 1) * CH].reshape(CH, CH)
+            u = lax.dot_general(ab[yy, t], w, NT, preferred_element_type=F32)
+            total = u if total is None else total + u
+        return total
+
+    def p_send(t):
+        return remote(pa.at[t], pr.at[t], ss_p.at[t], rs_p.at[t], d_l)
+
+    def p_away(t):
+        a_all(t)
+        pa[t] = partial(t, 1 - xl).astype(BF)
+        p_send(t).start()
+
+    def p_own(t):
+        pf[t] = partial(t, xl)
+
+    def o_send(t, i):
+        j, h = t // 2, t % 2
+        place = out.at[y, pl.ds(h * ROWS, ROWS), :]
+        return remote(rb.at[t, i], place, ss_o.at[t, i], rs_o.at[y, h], dev(z, xh, 2 * c + j, xl, i))
+
+    def o_here(t, i):
+        return jnp.logical_and(y == 2 * c + t // 2, c == i)
+
+    def p_got(t):
+        p_send(t).wait_recv()
+        h = t % 2
+        for i in range(2):
+            cols = slice(i * SH, (i + 1) * SH)
+            total = (pf[t, :, cols] + pr[t, :, cols].astype(F32)).astype(BF)
+
+            @pl.when(o_here(t, i))
+            def _():
+                out[y, h * ROWS : (h + 1) * ROWS, :] = total
+
+            @pl.when(jnp.logical_not(o_here(t, i)))
+            def _():
+                rb[t, i] = total
+                o_send(t, i).start()
 
     got_z1(0)
     got_z1(1)
     for h in range(2):
         w_ring(1, 0, h).start()
-    attend(0, diagonal(0) + [full(own.at[2], 4)], first=True)
-    w_got(0, 0)
-    attend(1, diagonal(1) + [full(own.at[2], 4)], first=True)
+    got_c(0)
+    w_got(0, 0, 0)
+    attend(0, diagonal(0) + [full(own.at[2], 4), full(oth.at[0], odd[0])], first=True)
+    w_got(0, 0, 1)
     got_a(0)
     got_z2(0)
-    got_c(0)
-    for j in range(2):
-        attend(j, [full(oth.at[0], odd[0])])
+    attend(1, diagonal(1) + [full(own.at[2], 4), full(oth.at[0], odd[0])], first=True)
     got_a(1)
     got_z2(1)
-    attend(0, [full(own.at[1], 2)] + far(0))
-    got_b(0)
+    w_got(0, 1, 0)
+    w_got(0, 1, 1)
     got_c(1)
     got_c(2)
-    attend(0, [full(oth.at[1], odd[1]), full(oth.at[2], odd[2])])
-    w_got(0, 1)
+    middle = [full(oth.at[1], odd[1]), full(oth.at[2], odd[2]), full(own.at[1], 2)]
+    attend(0, middle + far(0))
+    got_b(0)
+    w_got(0, 2, 0)
+    attend(1, middle + far(1))
     got_b(1)
-    attend(1, [full(own.at[1], 2)] + far(1))
+    w_got(0, 2, 1)
+    w_got(1, 0, 0)
     got_c(3)
     finish(0)
-    attend(1, [full(oth.at[1], odd[1]), full(oth.at[2], odd[2])])
+    a_start(0)
+    a_start(1)
+    w_got(1, 0, 1)
+    w_got(0, 3, 0)
     finish(1)
-    w_got(1, 0)
-    w_got(0, 2)
+    w_got(0, 3, 1)
+    w_got(1, 1, 0)
+    w_got(1, 1, 1)
     a_got(0)
-    w_got(1, 1)
-    w_got(0, 3)
+    a_start(2)
+    w_got(0, 4, 0)
     a_got(1)
-    w_got(0, 4)
+    a_start(3)
+    w_got(0, 4, 1)
     for k in range(8):
         w_core(k, z).wait_recv()
-
-    def partial(j, half, i):
-        total = None
-        zz = half * 4 + i * 2
-        for yy in range(4):
-            w = wb[yy // 2, pl.ds(zz, 2), :, :, (yy % 2) * CH : (yy % 2 + 1) * CH].reshape(SH, CH)
-            u = lax.dot_general(ab[yy, j], w, NT, preferred_element_type=F32)
-            total = u if total is None else total + u
-        return total
-
-    def p_send(j, i):
-        return remote(pa.at[j, i], pr.at[j, i], ss_p.at[j, i], rs_p.at[j, i], d_l)
-
-    def o_send(j, i):
-        return remote(rb.at[j, i], out.at[y], ss_o.at[j, i], rs_o.at[y], dev(z, xh, 2 * c + j, xl, i))
-
-    def o_here(j, i):
-        return jnp.logical_and(y == 2 * c + j, c == i)
-
-    for j in range(2):
-        for k in range(2):
-            a_relay(k, j).wait_recv()
-        for i in range(2):
-            pa[j, i] = partial(j, 1 - xl, i).astype(BF)
-            p_send(j, i).start()
-        for i in range(2):
-            pf[j, i] = partial(j, xl, i)
-    for j in range(2):
-        for i in range(2):
-            p_send(j, i).wait_recv()
-            total = (pf[j, i] + pr[j, i].astype(F32)).astype(BF)
-
-            @pl.when(o_here(j, i))
-            def _():
-                out[y] = total
-
-            @pl.when(jnp.logical_not(o_here(j, i)))
-            def _():
-                rb[j, i] = total
-                o_send(j, i).start()
+    p_away(0)
+    a_got(2)
+    p_own(0)
+    p_away(1)
+    p_own(1)
+    a_got(3)
+    p_got(0)
+    p_away(2)
+    p_own(2)
+    p_got(1)
+    p_away(3)
+    p_own(3)
+    p_got(2)
+    p_got(3)
 
     for yy in range(4):
         @pl.when(jnp.logical_not(jnp.logical_and(yy == y, c == y // 2)))
         def _():
-            remote(rb.at[0, 0], out.at[yy], ss_o.at[0, 0], rs_o.at[yy], d_c).wait_recv()
+            for h in range(2):
+                place = out.at[yy, pl.ds(h * ROWS, ROWS), :]
+                remote(rb.at[0, 0], place, ss_o.at[0, 0], rs_o.at[yy, h], d_c).wait_recv()
     for i in range(2):
         @pl.when(is_remote(i))
         def _():
@@ -371,16 +405,15 @@
             c_send(0, k, h).wait_send()
     for k in range(8):
         w_core(k, z).wait_send()
-    for j in range(2):
+    for t in range(4):
         for k in range(2):
-            a_send(k, j).wait_send()
-            a_relay(k, j).wait_send()
+            a_send(k, t).wait_send()
+            a_relay(k, t).wait_send()
+        p_send(t).wait_send()
         for i in range(2):
-            p_send(j, i).wait_send()
-
-            @pl.when(jnp.logical_not(o_here(j, i)))
+            @pl.when(jnp.logical_not(o_here(t, i)))
             def _():
-                o_send(j, i).wait_send()
+                o_send(t, i).wait_send()
 
 
 def body(queries, keys, values, out_weight):
@@ -388,7 +421,7 @@
     q = queries.reshape(tokens, 2, 4, HS).transpose(1, 2, 0, 3)
     kv = jnp.stack([keys, values]).transpose(2, 0, 1, 3)
     dma = pltpu.SemaphoreType.DMA
-    shapes = [(2,)] * 4 + [(2, 2)] * 4 + [(4, 2)] * 2 + [(1,)] * 2 + [(DOWN + UP, 2)] * 2 + [(8,)] * 2 + [(2, 2)] * 7 + [(4,)]
+    shapes = [(2,)] * 4 + [(2, 2)] * 4 + [(4, 2)] * 2 + [(1,)] * 2 + [(DOWN + UP, 2)] * 2 + [(8,)] * 2 + [(2, 4)] * 4 + [(4,)] * 2 + [(4, 2)] * 2
     sems = [dma(shape) for shape in shapes]
     vmem = pl.BlockSpec(memory_space=pltpu.VMEM)
     r = pl.pallas_call(
@@ -404,11 +437,11 @@
             pltpu.VMEM((2, 8, 2, 64, 1024), BF),
             pltpu.VMEM((2, 4, SH, HS), F32),
             pltpu.VMEM((2, 4, SH, 2 * HS), F32),
-            pltpu.VMEM((4, 2, SH, CH), BF),
-            pltpu.VMEM((2, 2, SH, SH), F32),
-            pltpu.VMEM((2, 2, SH, SH), BF),
-            pltpu.VMEM((2, 2, SH, SH), BF),
-            pltpu.VMEM((2, 2, SH, SH), BF),
+            pltpu.VMEM((4, 4, ROWS, CH), BF),
+            pltpu.VMEM((4, ROWS, CH), F32),
+            pltpu.VMEM((4, ROWS, CH), BF),
+            pltpu.VMEM((4, ROWS, CH), BF),
+            pltpu.VMEM((4, 2, ROWS, SH), BF),
             *sems,
         ],
         compiler_params=pltpu.CompilerParams(

time: 78.6 us -> 74.3 us (0.945)
  the two profiles are of different devices: /device:TPU:1 before, /device:TPU:9 now
where the time goes in v3:
time: 74.3 us; the launch traced here: 74.2 us
  Pallas kernels  70.9 us (95%)
  local copies, waits for them, and re-layouts  3.28 us (4%)
    pallas_call x1, Pallas kernels, body(): pl.pallas_call(kernel, name='layer', out_shape=jax.ShapeDtypeStruct((4, S...  70.9 us

profile of v3, /device:TPU:9, one launch (start us, length us, event | category | flops | bytes accessed | tf_op | source)
XLA Modules:
  0.0 74.2 jit_solution(2348404036566032606)
XLA Ops:
  0.0 0.0 copy-start.1
  0.0 1.1 %copy_bitcast_fusion = (bf16[1,256,2,128]{3,1,0,2:T(8,128)(2,1)S(1)}, bf16[1,256,2,128]{3,1,0,2:T(8,128)(2,1)S(1)}) fusion(bf16[256,2,128]{2,1,0:T(2,128)(2,1)} %param.6, bf16[256,2,128]{2,1,0:T(2,128)(2,1)} %param.5), kind=kLoop, calls=%fused_computation.1 | loop fusion | bytes 524288 | tf_op jit(solution)/shard_map/stack | solution.py:422
  1.1 0.1 copy-done.1
  1.2 0.0 copy-start
  1.2 0.1 copy.9
  1.2 0.8 %copy-done = bf16[1024,64]{0,1:T(8,128)(2,1)S(1)} copy-done((bf16[1024,64]{0,1:T(8,128)(2,1)S(1)}, bf16[1024,64]{0,1:T(8,128)(2,1)}, u32[]{:S(2)}) %copy-start) | copy-done | bytes 131096
  2.1 70.9 %layer.1 = bf16[4,256,256]{2,1,0:T(8,128)(2,1)S(1)} custom-call(bf16[2,4,256,128]{3,2,1,0:T(8,128)(2,1)S(1)} %bitcast.14, bf16[2,2,256,128]{3,2,1,0:T(8,128)(2,1)S(1)} %maximum_bitcast_fusion.kv_in, bf16[64,1024]{1,0:T(8,128)(2,1)S(1)} %bitcast.15), custom_call_target="tpu_custom_call" | custom-call | tf_op jit(solution)/shard_map/layer/pallas_call | solution.py:427
  73.0 0.2 copy.12
  73.2 1.0 %copy.14 = bf16[256,1024]{1,0:T(8,128)(2,1)} copy(bf16[256,1024]{0,1:T(8,128)(2,1)S(1)} %bitcast.17) | data formatting | bytes 1048576 | tf_op jit(solution)/shard_map/reshape | solution.py:451
  (2 shorter events, 0.1 us)
Async XLA Ops:
  0.0 1.2 %copy-start.1 = (bf16[256,8,128]{2,1,0:T(8,128)(2,1)S(1)}, bf16[256,8,128]{2,1,0:T(8,128)(2,1)}, u32[]{:S(2)}) copy-start(bf16[256,8,128]{2,1,0:T(8,128)(2,1)} %param.4) | copy-start | bytes 1572868
  1.2 0.9 %copy-start = (bf16[1024,64]{0,1:T(8,128)(2,1)S(1)}, bf16[1024,64]{0,1:T(8,128)(2,1)}, u32[]{:S(2)}) copy-start(bf16[1024,64]{0,1:T(8,128)(2,1)} %param.7) | copy-start | bytes 393220

commit v4 on v3

--- a/solution.py
+++ b/solution.py
@@ -15,7 +15,9 @@
 SH = 256
 CH = 512
 ROWS = 128
-DOWN, UP = 5, 2
+Q4 = 64
+RING = [(0, s, h) for s in range(5) for h in range(2) if (s, h) != (4, 1)]
+RING += [(1, s, h) for s in range(3) for h in range(2) if (s, h) != (2, 0)]
 BF = jnp.bfloat16
 F32 = jnp.float32
 
@@ -100,17 +102,17 @@
 
     w_x = remote(w_in, wb.at[c, z, xh], ss_wx.at[0], rs_wx.at[0], d_x)
     w_x.start()
+    wb[c, z, xh] = w_in[...]
     for i in range(2):
         @pl.when(is_remote(i))
         def _():
             to_head(i)[1].start()
 
+    for i in range(2):
         @pl.when(jnp.logical_not(is_remote(i)))
         def _():
             own[0, :, i * SH : (i + 1) * SH, :] = kv_in[i]
             qb[i] = q_in[i]
-
-    wb[c, z, xh] = w_in[...]
 
     def wait_in(which, j):
         @pl.when(jnp.logical_not(jnp.logical_and(mine_here, jy == j)))
@@ -121,8 +123,8 @@
                 remote(q_in.at[0], qb.at[j], ss_q.at[0], rs_q.at[j], d_c).wait_recv()
 
     def w_ring(k, s, h):
-        b = wb.at[c, lax.rem(z + s, 8) if k == 0 else lax.rem(z + 8 - s, 8), h]
-        n = s if k == 0 else DOWN + s
+        b = wb.at[c, lax.rem(z + s, 8) if k == 0 else lax.rem(z + 8 - s, 8), 1 - xh if h else xh]
+        n = s if k == 0 else 5 + s
         return remote(b, b, ss_w.at[n, h], rs_w.at[n, h], d_zp if k else d_zm)
 
     def w_core(n, block):
@@ -131,12 +133,11 @@
 
     def w_got(k, s, h):
         w_ring(k, s, h).wait_recv()
-        if s + 1 < (UP if k else DOWN):
+        if (k, s + 1, h) in RING:
             w_ring(k, s + 1, h).start()
-        if h == 1 and k == 0:
-            w_core(1 + s, lax.rem(z + 1 + s, 8)).start()
-        if h == 1 and k == 1:
-            w_core(1 + DOWN + s, lax.rem(z + 7 - s, 8)).start()
+        if h == 1 and s < (2 if k else 4):
+            n = 5 + s if k else 1 + s
+            w_core(n, lax.rem(z + 7 - s, 8) if k else lax.rem(z + 1 + s, 8)).start()
 
     def half(item, h):
         return own.at[item, :, pl.ds(h * SH, SH), :]
@@ -155,15 +156,17 @@
         def _():
             make(*args).start()
 
+    for k in range(2):
+        w_ring(k, 0, 0).start()
     for h in range(2):
         wait_in(0, h)
         z_send(0, h).start()
         start_if(xh == 0, x_send, 0, 0, h)
         start_if(c == 0, c_send, 0, 0, h)
     w_x.wait_recv()
-    for h in range(2):
-        w_ring(0, 0, h).start()
+    w_ring(0, 0, 1).start()
     w_core(0, z).start()
+    w_got(0, 0, 0)
     for j in range(2):
         wait_in(1, j)
 
@@ -199,16 +202,19 @@
     def bias(delta):
         return jnp.where(hg >= delta, 0.0, BIG).astype(F32)
 
-    ones = jnp.ones((CH, HS), BF)
-
-    def attend(j, segs, first=False):
-        for g in range(4):
-            for h in range(SH // ROWS):
-                rows = slice(h * ROWS, (h + 1) * ROWS)
-                q = qb[j, g, rows, :]
-                scores, tops = [], []
-                for ref, lo, size, mask, b in segs:
-                    s = lax.dot_general(q, ref[0, lo : lo + size, :], NT, preferred_element_type=F32)
+    def attend(h, segs_of, first=False):
+        rows = slice(h * ROWS, (h + 1) * ROWS)
+        for j in range(2):
+            segs = segs_of(j)
+            keys = jnp.concatenate([ref[0, lo : lo + size, :] for ref, lo, size, _, _ in segs], 0)
+            vals = jnp.concatenate([ref[1, lo : lo + size, :] for ref, lo, size, _, _ in segs], 0)
+            vals = jnp.concatenate([vals, jnp.ones(vals.shape, BF)], 1)
+            for g in range(4):
+                every = lax.dot_general(qb[j, g, rows, :], keys, NT, preferred_element_type=F32)
+                scores, tops, at = [], [], 0
+                for _, _, size, mask, b in segs:
+                    s = every[:, at : at + size]
+                    at += size
                     if mask is not None:
                         t = lax.broadcasted_iota(jnp.int32, s.shape, 0) + h * ROWS
                         k = lax.broadcasted_iota(jnp.int32, s.shape, 1)
@@ -216,21 +222,17 @@
                     m = jnp.max(s, axis=1, keepdims=True)
                     scores.append(s)
                     tops.append(m if b is None else m - b)
-                top = tops[0]
-                for m in tops[1:]:
-                    top = jnp.maximum(top, m)
+                top = functools.reduce(jnp.maximum, tops)
                 if first:
                     new = jnp.broadcast_to(top, (ROWS, HS))
                 else:
                     old = mx[j, g, rows, :]
                     new = jnp.maximum(old, top)
-                total = None
-                for s, (ref, lo, size, mask, b) in zip(scores, segs):
+                probs = []
+                for s, (_, _, _, _, b) in zip(scores, segs):
                     m = new[:, :1] if b is None else new[:, :1] + b
-                    p = jnp.exp2((s - m) * scale).astype(BF)
-                    v = jnp.concatenate([ref[1, lo : lo + size, :], ones[:size]], 1)
-                    u = jnp.dot(p, v, preferred_element_type=F32)
-                    total = u if total is None else total + u
+                    probs.append(jnp.exp2((s - m) * scale).astype(BF))
+                total = jnp.dot(jnp.concatenate(probs, 1), vals, preferred_element_type=F32)
                 if first:
                     acc[j, g, rows, :] = total
                 else:
@@ -274,13 +276,15 @@
         for k in range(2):
             a_relay(k, t).wait_recv()
 
-    def finish(j):
-        attend(j, [full(own.at[3], 6), full(oth.at[3], odd[3])])
-        for h in range(2):
-            rows = slice(h * ROWS, (h + 1) * ROWS)
+    def finish(h):
+        attend(h, lambda j: [full(own.at[3], 6), full(oth.at[3], odd[3])])
+        rows = slice(h * ROWS, (h + 1) * ROWS)
+        for j in range(2):
             for g in range(4):
                 a = acc[j, g, rows, :]
-                ab[y, 2 * j + h, :, g * HS : (g + 1) * HS] = (a[:, :HS] / a[:, HS:]).astype(BF)
+                a = (a[:, :HS] / a[:, HS:]).astype(BF)
+                for t in range(2):
+                    ab[y, 2 * h + t, j * Q4 : (j + 1) * Q4, g * HS : (g + 1) * HS] = a[t * Q4 : (t + 1) * Q4]
 
     def partial(t, side):
         total = None
@@ -301,76 +305,78 @@
     def p_own(t):
         pf[t] = partial(t, xl)
 
-    def o_send(t, i):
-        j, h = t // 2, t % 2
-        place = out.at[y, pl.ds(h * ROWS, ROWS), :]
-        return remote(rb.at[t, i], place, ss_o.at[t, i], rs_o.at[y, h], dev(z, xh, 2 * c + j, xl, i))
-
-    def o_here(t, i):
-        return jnp.logical_and(y == 2 * c + t // 2, c == i)
+    def o_send(t, j, i):
+        place = out.at[y, pl.ds(t * Q4, Q4), :]
+        return remote(rb.at[t, i, pl.ds(j * Q4, Q4), :], place, ss_o.at[t, 2 * j + i], rs_o.at[y, t], dev(z, xh, 2 * c + j, xl, i))
+
+    def o_here(j, i):
+        return jnp.logical_and(y == 2 * c + j, c == i)
 
     def p_got(t):
         p_send(t).wait_recv()
-        h = t % 2
         for i in range(2):
             cols = slice(i * SH, (i + 1) * SH)
-            total = (pf[t, :, cols] + pr[t, :, cols].astype(F32)).astype(BF)
-
-            @pl.when(o_here(t, i))
-            def _():
-                out[y, h * ROWS : (h + 1) * ROWS, :] = total
-
-            @pl.when(jnp.logical_not(o_here(t, i)))
-            def _():
-                rb[t, i] = total
-                o_send(t, i).start()
+            rb[t, i] = (pf[t, :, cols] + pr[t, :, cols].astype(F32)).astype(BF)
+        for j in range(2):
+            for i in range(2):
+                @pl.when(o_here(j, i))
+                def _():
+                    out[y, t * Q4 : (t + 1) * Q4, :] = rb[t, i, j * Q4 : (j + 1) * Q4, :]
+
+                @pl.when(jnp.logical_not(o_here(j, i)))
+                def _():
+                    o_send(t, j, i).start()
+
+    def near(j):
+        return diagonal(j) + [full(own.at[2], 4), full(oth.at[0], odd[0])]
+
+    def middle(j):
+        return [full(own.at[1], 2), full(oth.at[1], odd[1]), full(oth.at[2], odd[2])] + far(j)
 
     got_z1(0)
     got_z1(1)
-    for h in range(2):
-        w_ring(1, 0, h).start()
+    w_ring(1, 0, 1).start()
+    w_got(1, 0, 0)
+    w_got(0, 0, 1)
     got_c(0)
-    w_got(0, 0, 0)
-    attend(0, diagonal(0) + [full(own.at[2], 4), full(oth.at[0], odd[0])], first=True)
-    w_got(0, 0, 1)
+    attend(0, near, first=True)
+    w_got(0, 1, 0)
     got_a(0)
     got_z2(0)
-    attend(1, diagonal(1) + [full(own.at[2], 4), full(oth.at[0], odd[0])], first=True)
+    w_got(0, 1, 1)
+    attend(1, near, first=True)
     got_a(1)
     got_z2(1)
-    w_got(0, 1, 0)
-    w_got(0, 1, 1)
+    w_got(0, 2, 0)
     got_c(1)
     got_c(2)
-    middle = [full(oth.at[1], odd[1]), full(oth.at[2], odd[2]), full(own.at[1], 2)]
-    attend(0, middle + far(0))
+    attend(0, middle)
     got_b(0)
-    w_got(0, 2, 0)
-    attend(1, middle + far(1))
     got_b(1)
     w_got(0, 2, 1)
-    w_got(1, 0, 0)
+    w_got(1, 0, 1)
+    w_got(1, 1, 0)
+    w_got(0, 3, 0)
     got_c(3)
     finish(0)
     a_start(0)
     a_start(1)
-    w_got(1, 0, 1)
-    w_got(0, 3, 0)
+    w_got(1, 1, 1)
+    attend(1, middle)
+    w_got(0, 3, 1)
+    w_got(0, 4, 0)
+    a_got(0)
     finish(1)
-    w_got(0, 3, 1)
-    w_got(1, 1, 0)
-    w_got(1, 1, 1)
-    a_got(0)
     a_start(2)
-    w_got(0, 4, 0)
     a_got(1)
     a_start(3)
-    w_got(0, 4, 1)
+    w_got(1, 2, 1)
+    w_core(7, lax.rem(z + 5, 8)).start()
     for k in range(8):
         w_core(k, z).wait_recv()
     p_away(0)
+    p_own(0)
     a_got(2)
-    p_own(0)
     p_away(1)
     p_own(1)
     a_got(3)
@@ -386,19 +392,19 @@
     for yy in range(4):
         @pl.when(jnp.logical_not(jnp.logical_and(yy == y, c == y // 2)))
         def _():
-            for h in range(2):
-                place = out.at[yy, pl.ds(h * ROWS, ROWS), :]
-                remote(rb.at[0, 0], place, ss_o.at[0, 0], rs_o.at[yy, h], d_c).wait_recv()
+            for t in range(4):
+                place = out.at[yy, pl.ds(t * Q4, Q4), :]
+                remote(rb.at[0, 0, pl.ds(0, Q4), :], place, ss_o.at[0, 0], rs_o.at[yy, t], d_c).wait_recv()
     for i in range(2):
         @pl.when(is_remote(i))
         def _():
             for copy in to_head(i):
                 copy.wait_send()
     w_x.wait_send()
+    for k, n, h in RING:
+        w_ring(k, n, h).wait_send()
     for h in range(2):
         for k in range(2):
-            for n in range(UP if k else DOWN):
-                w_ring(k, n, h).wait_send()
             z_send(k, h).wait_send()
             x_send(0, k, h).wait_send()
         for k in range(4):
@@ -410,10 +416,11 @@
             a_send(k, t).wait_send()
             a_relay(k, t).wait_send()
         p_send(t).wait_send()
-        for i in range(2):
-            @pl.when(jnp.logical_not(o_here(t, i)))
-            def _():
-                o_send(t, i).wait_send()
+        for j in range(2):
+            for i in range(2):
+                @pl.when(jnp.logical_not(o_here(j, i)))
+                def _():
+                    o_send(t, j, i).wait_send()
 
 
 def body(queries, keys, values, out_weight):
@@ -421,7 +428,7 @@
     q = queries.reshape(tokens, 2, 4, HS).transpose(1, 2, 0, 3)
     kv = jnp.stack([keys, values]).transpose(2, 0, 1, 3)
     dma = pltpu.SemaphoreType.DMA
-    shapes = [(2,)] * 4 + [(2, 2)] * 4 + [(4, 2)] * 2 + [(1,)] * 2 + [(DOWN + UP, 2)] * 2 + [(8,)] * 2 + [(2, 4)] * 4 + [(4,)] * 2 + [(4, 2)] * 2
+    shapes = [(2,)] * 4 + [(2, 2)] * 4 + [(4, 2)] * 2 + [(1,)] * 2 + [(8, 2)] * 2 + [(8,)] * 2 + [(2, 4)] * 4 + [(4,)] * 2 + [(4, 4)] * 2
     sems = [dma(shape) for shape in shapes]
     vmem = pl.BlockSpec(memory_space=pltpu.VMEM)
     r = pl.pallas_call(

time: 74.3 us -> 73 us (0.983)
  the two profiles are of different devices: /device:TPU:9 before, /device:TPU:1 now
where the time goes in v4:
time: 73 us; the launch traced here: 72.9 us
  Pallas kernels  69.6 us (95%)
  local copies, waits for them, and re-layouts  3.28 us (4%)
    pallas_call x1, Pallas kernels, body(): pl.pallas_call(kernel, name='layer', out_shape=jax.ShapeDtypeStruct((4, S...  69.6 us

profile of v4, /device:TPU:1, one launch (start us, length us, event | category | flops | bytes accessed | tf_op | source)
XLA Modules:
  0.0 72.9 jit_solution(2789412130135449056)
XLA Ops:
  0.0 0.0 copy-start.1
  0.0 1.1 %copy_bitcast_fusion = (bf16[1,256,2,128]{3,1,0,2:T(8,128)(2,1)S(1)}, bf16[1,256,2,128]{3,1,0,2:T(8,128)(2,1)S(1)}) fusion(bf16[256,2,128]{2,1,0:T(2,128)(2,1)} %param.6, bf16[256,2,128]{2,1,0:T(2,128)(2,1)} %param.5), kind=kLoop, calls=%fused_computation.1 | loop fusion | bytes 524288 | tf_op jit(solution)/shard_map/stack | solution.py:429
  1.1 0.1 copy-done.1
  1.2 0.0 copy-start
  1.2 0.1 copy.9
  1.2 0.8 %copy-done = bf16[1024,64]{0,1:T(8,128)(2,1)S(1)} copy-done((bf16[1024,64]{0,1:T(8,128)(2,1)S(1)}, bf16[1024,64]{0,1:T(8,128)(2,1)}, u32[]{:S(2)}) %copy-start) | copy-done | bytes 131096
  2.1 69.6 %layer.1 = bf16[4,256,256]{2,1,0:T(8,128)(2,1)S(1)} custom-call(bf16[2,4,256,128]{3,2,1,0:T(8,128)(2,1)S(1)} %bitcast.14, bf16[2,2,256,128]{3,2,1,0:T(8,128)(2,1)S(1)} %maximum_bitcast_fusion.kv_in, bf16[64,1024]{1,0:T(8,128)(2,1)S(1)} %bitcast.15), custom_call_target="tpu_custom_call" | custom-call | tf_op jit(solution)/shard_map/layer/pallas_call | solution.py:434
  71.6 0.2 copy.12
  71.9 1.0 %copy.14 = bf16[256,1024]{1,0:T(8,128)(2,1)} copy(bf16[256,1024]{0,1:T(8,128)(2,1)S(1)} %bitcast.17) | data formatting | bytes 1048576 | tf_op jit(solution)/shard_map/reshape | solution.py:458
  (2 shorter events, 0.1 us)
Async XLA Ops:
  0.0 1.2 %copy-start.1 = (bf16[256,8,128]{2,1,0:T(8,128)(2,1)S(1)}, bf16[256,8,128]{2,1,0:T(8,128)(2,1)}, u32[]{:S(2)}) copy-start(bf16[256,8,128]{2,1,0:T(8,128)(2,1)} %param.4) | copy-start | bytes 1572868
  1.2 0.9 %copy-start = (bf16[1024,64]{0,1:T(8,128)(2,1)S(1)}, bf16[1024,64]{0,1:T(8,128)(2,1)}, u32[]{:S(2)}) copy-start(bf16[1024,64]{0,1:T(8,128)(2,1)} %param.7) | copy-start | bytes 393220

commit v5 on v4

--- a/solution.py
+++ b/solution.py
@@ -15,7 +15,7 @@
 SH = 256
 CH = 512
 ROWS = 128
-Q4 = 64
+PIECES = [(0, 0, 64), (0, 64, 64), (1, 128, 64), (1, 192, 32), (1, 224, 32)]
 RING = [(0, s, h) for s in range(5) for h in range(2) if (s, h) != (4, 1)]
 RING += [(1, s, h) for s in range(3) for h in range(2) if (s, h) != (2, 0)]
 BF = jnp.bfloat16
@@ -255,12 +255,17 @@
 
     yp, ym = lax.rem(y + 1, 4), lax.rem(y + 3, 4)
 
+    def piece(t):
+        _, lo, n = PIECES[t]
+        return slice(2 * lo, 2 * (lo + n)), pl.ds(2 * lo, 2 * n)
+
     def a_send(k, t):
-        b = ab.at[y, t]
+        b = ab.at[y, piece(t)[1], :]
         return remote(b, b, ss_a.at[k, t], rs_a.at[k, t], dev(z, xh, ym if k else yp, xl, c))
 
     def a_relay(k, t):
-        b = ab.at[yp if k else ym, t, pl.ds(k * 64, 64), :]
+        _, lo, n = PIECES[t]
+        b = ab.at[yp if k else ym, pl.ds(2 * lo + k * n, n), :]
         return remote(b, b, ss_r.at[k, t], rs_r.at[k, t], dev(z, xh, ym if k else yp, xl, c))
 
     def a_start(t):
@@ -283,45 +288,51 @@
             for g in range(4):
                 a = acc[j, g, rows, :]
                 a = (a[:, :HS] / a[:, HS:]).astype(BF)
-                for t in range(2):
-                    ab[y, 2 * h + t, j * Q4 : (j + 1) * Q4, g * HS : (g + 1) * HS] = a[t * Q4 : (t + 1) * Q4]
+                for p, lo, n in PIECES:
+                    if p == h:
+                        row, tok = 2 * lo + j * n, lo - h * ROWS
+                        ab[y, row : row + n, g * HS : (g + 1) * HS] = a[tok : tok + n]
 
     def partial(t, side):
         total = None
         for yy in range(4):
             w = wb[yy // 2, pl.ds(side * 4, 4), :, :, (yy % 2) * CH : (yy % 2 + 1) * CH].reshape(CH, CH)
-            u = lax.dot_general(ab[yy, t], w, NT, preferred_element_type=F32)
+            u = lax.dot_general(ab[yy, piece(t)[0], :], w, NT, preferred_element_type=F32)
             total = u if total is None else total + u
         return total
 
     def p_send(t):
-        return remote(pa.at[t], pr.at[t], ss_p.at[t], rs_p.at[t], d_l)
+        rows = piece(t)[1]
+        return remote(pa.at[rows, :], pr.at[rows, :], ss_p.at[t], rs_p.at[t], d_l)
 
     def p_away(t):
         a_all(t)
-        pa[t] = partial(t, 1 - xl).astype(BF)
+        pa[piece(t)[0], :] = partial(t, 1 - xl).astype(BF)
         p_send(t).start()
 
     def p_own(t):
-        pf[t] = partial(t, xl)
+        pf[piece(t)[0], :] = partial(t, xl)
 
     def o_send(t, j, i):
-        place = out.at[y, pl.ds(t * Q4, Q4), :]
-        return remote(rb.at[t, i, pl.ds(j * Q4, Q4), :], place, ss_o.at[t, 2 * j + i], rs_o.at[y, t], dev(z, xh, 2 * c + j, xl, i))
+        _, lo, n = PIECES[t]
+        source, place = rb.at[i, pl.ds(2 * lo + j * n, n), :], out.at[y, pl.ds(lo, n), :]
+        return remote(source, place, ss_o.at[t, 2 * j + i], rs_o.at[y, t], dev(z, xh, 2 * c + j, xl, i))
 
     def o_here(j, i):
         return jnp.logical_and(y == 2 * c + j, c == i)
 
     def p_got(t):
         p_send(t).wait_recv()
+        rows = piece(t)[0]
+        _, lo, n = PIECES[t]
         for i in range(2):
             cols = slice(i * SH, (i + 1) * SH)
-            rb[t, i] = (pf[t, :, cols] + pr[t, :, cols].astype(F32)).astype(BF)
+            rb[i, rows, :] = (pf[rows, cols] + pr[rows, cols].astype(F32)).astype(BF)
         for j in range(2):
             for i in range(2):
                 @pl.when(o_here(j, i))
                 def _():
-                    out[y, t * Q4 : (t + 1) * Q4, :] = rb[t, i, j * Q4 : (j + 1) * Q4, :]
+                    out[y, lo : lo + n, :] = rb[i, 2 * lo + j * n : 2 * lo + (j + 1) * n, :]
 
                 @pl.when(jnp.logical_not(o_here(j, i)))
                 def _():
@@ -361,13 +372,13 @@
     finish(0)
     a_start(0)
     a_start(1)
+    attend(1, middle)
     w_got(1, 1, 1)
-    attend(1, middle)
     w_got(0, 3, 1)
+    finish(1)
+    a_got(0)
+    a_start(2)
     w_got(0, 4, 0)
-    a_got(0)
-    finish(1)
-    a_start(2)
     a_got(1)
     a_start(3)
     w_got(1, 2, 1)
@@ -377,24 +388,28 @@
     p_away(0)
     p_own(0)
     a_got(2)
+    a_start(4)
     p_away(1)
+    a_got(3)
     p_own(1)
-    a_got(3)
     p_got(0)
     p_away(2)
+    a_got(4)
     p_own(2)
-    p_got(1)
     p_away(3)
     p_own(3)
-    p_got(2)
-    p_got(3)
+    p_got(1)
+    p_away(4)
+    p_own(4)
+    for t in range(2, 5):
+        p_got(t)
 
     for yy in range(4):
         @pl.when(jnp.logical_not(jnp.logical_and(yy == y, c == y // 2)))
         def _():
-            for t in range(4):
-                place = out.at[yy, pl.ds(t * Q4, Q4), :]
-                remote(rb.at[0, 0, pl.ds(0, Q4), :], place, ss_o.at[0, 0], rs_o.at[yy, t], d_c).wait_recv()
+            for t, (_, lo, n) in enumerate(PIECES):
+                place = out.at[yy, pl.ds(lo, n), :]
+                remote(rb.at[0, pl.ds(lo, n), :], place, ss_o.at[0, 0], rs_o.at[yy, t], d_c).wait_recv()
     for i in range(2):
         @pl.when(is_remote(i))
         def _():
@@ -411,7 +426,7 @@
             c_send(0, k, h).wait_send()
     for k in range(8):
         w_core(k, z).wait_send()
-    for t in range(4):
+    for t in range(len(PIECES)):
         for k in range(2):
             a_send(k, t).wait_send()
             a_relay(k, t).wait_send()
@@ -428,7 +443,7 @@
     q = queries.reshape(tokens, 2, 4, HS).transpose(1, 2, 0, 3)
     kv = jnp.stack([keys, values]).transpose(2, 0, 1, 3)
     dma = pltpu.SemaphoreType.DMA
-    shapes = [(2,)] * 4 + [(2, 2)] * 4 + [(4, 2)] * 2 + [(1,)] * 2 + [(8, 2)] * 2 + [(8,)] * 2 + [(2, 4)] * 4 + [(4,)] * 2 + [(4, 4)] * 2
+    shapes = [(2,)] * 4 + [(2, 2)] * 4 + [(4, 2)] * 2 + [(1,)] * 2 + [(8, 2)] * 2 + [(8,)] * 2 + [(2, 5)] * 4 + [(5,)] * 2 + [(5, 4), (4, 5)]
     sems = [dma(shape) for shape in shapes]
     vmem = pl.BlockSpec(memory_space=pltpu.VMEM)
     r = pl.pallas_call(
@@ -444,11 +459,11 @@
             pltpu.VMEM((2, 8, 2, 64, 1024), BF),
             pltpu.VMEM((2, 4, SH, HS), F32),
             pltpu.VMEM((2, 4, SH, 2 * HS), F32),
-            pltpu.VMEM((4, 4, ROWS, CH), BF),
-            pltpu.VMEM((4, ROWS, CH), F32),
-            pltpu.VMEM((4, ROWS, CH), BF),
-            pltpu.VMEM((4, ROWS, CH), BF),
-            pltpu.VMEM((4, 2, ROWS, SH), BF),
+            pltpu.VMEM((4, CH, CH), BF),
+            pltpu.VMEM((CH, CH), F32),
+            pltpu.VMEM((CH, CH), BF),
+            pltpu.VMEM((CH, CH), BF),
+            pltpu.VMEM((2, CH, SH), BF),
             *sems,
         ],
         compiler_params=pltpu.CompilerParams(

time: 73 us -> 71.5 us (0.979)
  Pallas kernels: 69.6 us -> 68.1 us
    pallas_call x1, Pallas kernels: 69.6 us -> 68.1 us  [body(): pl.pallas_call(kernel, name='layer', out_shape=jax.ShapeDtypeStruct((4, S...]
where the time goes in v5:
time: 71.5 us; the launch traced here: 71.4 us
  Pallas kernels  68.1 us (95%)
  local copies, waits for them, and re-layouts  3.28 us (5%)
    pallas_call x1, Pallas kernels, body(): pl.pallas_call(kernel, name='layer', out_shape=jax.ShapeDtypeStruct((4, S...  68.1 us

profile of v5, /device:TPU:1, one launch (start us, length us, event | category | flops | bytes accessed | tf_op | source)
XLA Modules:
  0.0 71.4 jit_solution(11896194680736432939)
XLA Ops:
  0.0 0.0 copy-start.1
  0.0 1.1 %copy_bitcast_fusion = (bf16[1,256,2,128]{3,1,0,2:T(8,128)(2,1)S(1)}, bf16[1,256,2,128]{3,1,0,2:T(8,128)(2,1)S(1)}) fusion(bf16[256,2,128]{2,1,0:T(2,128)(2,1)} %param.6, bf16[256,2,128]{2,1,0:T(2,128)(2,1)} %param.5), kind=kLoop, calls=%fused_computation.1 | loop fusion | bytes 524288 | tf_op jit(solution)/shard_map/stack | solution.py:444
  1.1 0.1 copy-done.1
  1.2 0.0 copy-start
  1.2 0.1 copy.9
  1.2 0.8 %copy-done = bf16[1024,64]{0,1:T(8,128)(2,1)S(1)} copy-done((bf16[1024,64]{0,1:T(8,128)(2,1)S(1)}, bf16[1024,64]{0,1:T(8,128)(2,1)}, u32[]{:S(2)}) %copy-start) | copy-done | bytes 131096
  2.1 68.1 %layer.1 = bf16[4,256,256]{2,1,0:T(8,128)(2,1)S(1)} custom-call(bf16[2,4,256,128]{3,2,1,0:T(8,128)(2,1)S(1)} %bitcast.14, bf16[2,2,256,128]{3,2,1,0:T(8,128)(2,1)S(1)} %maximum_bitcast_fusion.kv_in, bf16[64,1024]{1,0:T(8,128)(2,1)S(1)} %bitcast.15), custom_call_target="tpu_custom_call" | custom-call | tf_op jit(solution)/shard_map/layer/pallas_call | solution.py:449
  70.1 0.2 copy.12
  70.4 1.0 %copy.14 = bf16[256,1024]{1,0:T(8,128)(2,1)} copy(bf16[256,1024]{0,1:T(8,128)(2,1)S(1)} %bitcast.17) | data formatting | bytes 1048576 | tf_op jit(solution)/shard_map/reshape | solution.py:473
  (2 shorter events, 0.1 us)
Async XLA Ops:
  0.0 1.2 %copy-start.1 = (bf16[256,8,128]{2,1,0:T(8,128)(2,1)S(1)}, bf16[256,8,128]{2,1,0:T(8,128)(2,1)}, u32[]{:S(2)}) copy-start(bf16[256,8,128]{2,1,0:T(8,128)(2,1)} %param.4) | copy-start | bytes 1572868
  1.2 0.9 %copy-start = (bf16[1024,64]{0,1:T(8,128)(2,1)S(1)}, bf16[1024,64]{0,1:T(8,128)(2,1)}, u32[]{:S(2)}) copy-start(bf16[1024,64]{0,1:T(8,128)(2,1)} %param.7) | copy-start | bytes 393220

commit v6 on v5

--- a/solution.py
+++ b/solution.py
@@ -379,10 +379,10 @@
     a_got(0)
     a_start(2)
     w_got(0, 4, 0)
+    w_got(1, 2, 1)
+    w_core(7, lax.rem(z + 5, 8)).start()
     a_got(1)
     a_start(3)
-    w_got(1, 2, 1)
-    w_core(7, lax.rem(z + 5, 8)).start()
     for k in range(8):
         w_core(k, z).wait_recv()
     p_away(0)

time: 71.5 us -> 71.4 us (level)
  no operation moved by 1% of the time
where the time goes in v6:
time: 71.4 us; the launch traced here: 71.3 us
  Pallas kernels  67.9 us (95%)
  local copies, waits for them, and re-layouts  3.28 us (5%)
    pallas_call x1, Pallas kernels, body(): pl.pallas_call(kernel, name='layer', out_shape=jax.ShapeDtypeStruct((4, S...  67.9 us

profile of v6, /device:TPU:1, one launch (start us, length us, event | category | flops | bytes accessed | tf_op | source)
XLA Modules:
  0.0 71.3 jit_solution(6678073164406689048)
XLA Ops:
  0.0 0.0 copy-start.1
  0.0 1.1 %copy_bitcast_fusion = (bf16[1,256,2,128]{3,1,0,2:T(8,128)(2,1)S(1)}, bf16[1,256,2,128]{3,1,0,2:T(8,128)(2,1)S(1)}) fusion(bf16[256,2,128]{2,1,0:T(2,128)(2,1)} %param.6, bf16[256,2,128]{2,1,0:T(2,128)(2,1)} %param.5), kind=kLoop, calls=%fused_computation.1 | loop fusion | bytes 524288 | tf_op jit(solution)/shard_map/stack | solution.py:444
  1.1 0.1 copy-done.1
  1.2 0.0 copy-start
  1.2 0.1 copy.9
  1.2 0.8 %copy-done = bf16[1024,64]{0,1:T(8,128)(2,1)S(1)} copy-done((bf16[1024,64]{0,1:T(8,128)(2,1)S(1)}, bf16[1024,64]{0,1:T(8,128)(2,1)}, u32[]{:S(2)}) %copy-start) | copy-done | bytes 131096
  2.1 67.9 %layer.1 = bf16[4,256,256]{2,1,0:T(8,128)(2,1)S(1)} custom-call(bf16[2,4,256,128]{3,2,1,0:T(8,128)(2,1)S(1)} %bitcast.14, bf16[2,2,256,128]{3,2,1,0:T(8,128)(2,1)S(1)} %maximum_bitcast_fusion.kv_in, bf16[64,1024]{1,0:T(8,128)(2,1)S(1)} %bitcast.15), custom_call_target="tpu_custom_call" | custom-call | tf_op jit(solution)/shard_map/layer/pallas_call | solution.py:449
  70.0 0.2 copy.12
  70.3 1.0 %copy.14 = bf16[256,1024]{1,0:T(8,128)(2,1)} copy(bf16[256,1024]{0,1:T(8,128)(2,1)S(1)} %bitcast.17) | data formatting | bytes 1048576 | tf_op jit(solution)/shard_map/reshape | solution.py:473
  (2 shorter events, 0.1 us)
Async XLA Ops:
  0.0 1.2 %copy-start.1 = (bf16[256,8,128]{2,1,0:T(8,128)(2,1)S(1)}, bf16[256,8,128]{2,1,0:T(8,128)(2,1)}, u32[]{:S(2)}) copy-start(bf16[256,8,128]{2,1,0:T(8,128)(2,1)} %param.4) | copy-start | bytes 1572868
  1.2 0.9 %copy-start = (bf16[1024,64]{0,1:T(8,128)(2,1)S(1)}, bf16[1024,64]{0,1:T(8,128)(2,1)}, u32[]{:S(2)}) copy-start(bf16[1024,64]{0,1:T(8,128)(2,1)} %param.7) | copy-start | bytes 393220
